TPU v7x, 8 devices: a whole 2x2x1 slice. The times are simulated.
8 devices in a mesh: col: 4 (over z, y, x), row: 2 (over core).
Axes of the slice: x: 2, y: 2, z: 1, core: 2. Of those that a mesh axis runs over, the one named last changes fastest.
Arguments:
- mask: int32 [4096, 65536], P('row', 'col')
- user_emb: bfloat16 [4096, 256], P(('row', 'col'))
- item_emb: bfloat16 [65536, 256], P(('col', 'row'))
- queries: int32 [512], replicated
Outputs:
- output 1: bfloat16 [4096, 256], P(('row', 'col'))
- output 2: bfloat16 [65536, 256], P(('col', 'row'))
- output 3: float32 [512, 65536], P(None, ('col', 'row'))
All inputs are finite; a program needn't handle non-finite values.
Results may differ from a plain program's by a relative error of at most 0.00683025.
Values are sent between devices in bfloat16 or wider.
A program may use at most 1 GiB of HBM per device.

v0:
```python
import jax
import jax.numpy as jnp
from jax import lax
from jax.sharding import PartitionSpec as P

LAYERS = 3


def norm_block(mask_blk):
    deg_user = lax.psum(jnp.sum(mask_blk, axis=1), 'col')
    deg_item = lax.psum(jnp.sum(mask_blk, axis=0), 'row')
    inv_user = lax.rsqrt(jnp.maximum(deg_user, 1).astype(jnp.float32))
    inv_item = lax.rsqrt(jnp.maximum(deg_item, 1).astype(jnp.float32))
    return (inv_user[:, None] * mask_blk.astype(jnp.float32) * inv_item[None, :]).astype(jnp.bfloat16)


def query_scores(final_user, final_item, queries, shard_pos):
    rows_local = final_user.shape[0]
    local_idx = queries - shard_pos * rows_local
    owned = (local_idx >= 0) & (local_idx < rows_local)
    picked = jnp.take(final_user, jnp.clip(local_idx, 0, rows_local - 1), axis=0)
    picked = jnp.where(owned[:, None], picked, jnp.zeros_like(picked))
    picked = lax.psum(picked, ('row', 'col'))
    return lax.dot_general(picked, final_item, (((1,), (1,)), ((), ())), preferred_element_type=jnp.float32)


def solution(mesh):
    n_col = mesh.shape['col']
    contract_rows = (((0,), (0,)), ((), ()))

    def device_step(mask_blk, user_shard, item_shard, queries):
        norm_adj = norm_block(mask_blk)
        user_cur = user_shard
        item_cur = item_shard
        user_sum = user_shard.astype(jnp.float32)
        item_sum = item_shard.astype(jnp.float32)
        for layer_idx in range(LAYERS):
            item_panel = lax.all_gather(item_cur, 'row', axis=0, tiled=True)
            user_part = jnp.dot(norm_adj, item_panel, preferred_element_type=jnp.float32)
            user_next = lax.psum_scatter(user_part, 'col', scatter_dimension=0, tiled=True).astype(jnp.bfloat16)
            user_panel = lax.all_gather(user_cur, 'col', axis=0, tiled=True)
            item_part = lax.dot_general(norm_adj, user_panel, contract_rows, preferred_element_type=jnp.float32)
            item_next = lax.psum_scatter(item_part, 'row', scatter_dimension=0, tiled=True).astype(jnp.bfloat16)
            user_sum = user_sum + user_next.astype(jnp.float32)
            item_sum = item_sum + item_next.astype(jnp.float32)
            user_cur = user_next
            item_cur = item_next
        final_user = (user_sum / (LAYERS + 1)).astype(jnp.bfloat16)
        final_item = (item_sum / (LAYERS + 1)).astype(jnp.bfloat16)
        shard_pos = lax.axis_index('row') * n_col + lax.axis_index('col')
        scores = query_scores(final_user, final_item, queries, shard_pos)
        return final_user, final_item, scores

    return jax.shard_map(device_step, mesh=mesh, in_specs=(P('row', 'col'), P(('row', 'col'), None), P(('col', 'row'), None), P()), out_specs=(P(('row', 'col'), None), P(('col', 'row'), None), P(None, ('col', 'row'))), check_vma=False)
```

profile of v0, /device:TPU:0, one launch (start us, length us, event | category | flops | bytes accessed | tf_op | source)
XLA Modules:
  0.0 566.7 jit_solution(1032675281737103169)
XLA Ops:
  8.0 0.0 all-reduce.3.cloned.1.call-start
  8.0 40.8 %fusion = (s32[2048]{0:T(1024)S(1)}, s32[16384]{0:T(1024)}) fusion(s32[2048,16384]{1,0:T(8,128)} %param.4), kind=kLoop, calls=%fused_computation.11 | loop fusion | flops 67090432 | bytes 134291456 | tf_op jit(solution)/shard_map/reduce_sum | solution.py:10
  48.8 0.0 all-gather.9.cloned.1.call-start
  48.9 0.5 all-gather.9.cloned.1.call-update
  49.4 0.0 reduce-scatter.9.cloned.1.call-start
  49.4 9.4 %psum.21 = s32[2048]{0:T(1024)S(1)} all-reduce(s32[2048]{0:T(1024)S(1)} %get-tuple-element.3), channel_id=1, replica_groups=mesh['col'=4,'row'=2] {'col'}, use_global_device_ids=true, to_apply=%region_1.0 | all-reduce | flops 2048 | bytes 16384 | tf_op jit(solution)/shard_map/psum | solution.py:10
  58.8 5.0 all-reduce.3.cloned.1.call-done
  63.8 0.9 convert_rsqrt_fusion
  64.7 64.1 %multiply_convert_fusion = bf16[2048,16384]{1,0:T(8,128)(2,1)} fusion(s32[2048,16384]{1,0:T(8,128)} %param.4, f32[16384]{0:T(1024)S(1)} %convert_rsqrt_fusion, f32[2048]{0:T(1024)S(1)} %convert_rsqrt_fusion.1), kind=kLoop, calls=%fused_computation.1 | loop fusion | flops 134217728 | bytes 201400320 | tf_op jit(solution)/shard_map/convert_element_type | solution.py:14
  128.8 31.8 %fusion.2 = f32[16384,256]{1,0:T(8,128)} fusion(bf16[2048,16384]{1,0:T(8,128)(2,1)} %multiply_convert_fusion, bf16[2048,256]{1,0:T(8,128)(2,1)} %all-gather.9.cloned.1.call-done), kind=kOutput, calls=%fused_computation.13 | convolution fusion | flops 17179869184 | bytes 84934656 | tf_op jit(solution)/shard_map/dot_general | solution.py:42
  160.7 0.0 all-gather.7.cloned.1.call-start
  160.7 0.7 all-gather.7.cloned.1.call-update
  161.4 0.0 all-gather.11.cloned.1.call-start
  161.5 22.4 %reduce-scatter.9.cloned.1.call-done = f32[8192,256]{1,0:T(8,128)} async-done(((f32[16384,256]{1,0:T(8,128)}), f32[8192,256]{1,0:T(8,128)}) %reduce-scatter.9.cloned.1.call-update) | async-done | bytes 8388624 | tf_op jit(solution)/shard_map/reduce_scatter | solution.py:43
  183.9 5.8 %convert_element_type.67 = bf16[8192,256]{1,0:T(8,128)(2,1)} convert(f32[8192,256]{1,0:T(8,128)} %reduce-scatter.9.cloned.1.call-done) | non-fusion elementwise | flops 2097152 | bytes 12582912 | tf_op jit(solution)/shard_map/convert_element_type | solution.py:43
  189.7 0.2 reduce-scatter.7.cloned.1.call-start
  189.9 14.6 %all-gather.7.cloned.1.call-done = bf16[16384,256]{1,0:T(8,128)(2,1)} async-done(((bf16[8192,256]{1,0:T(8,128)(2,1)}), bf16[16384,256]{1,0:T(8,128)(2,1)}) %all-gather.7.cloned.1.call-update) | async-done | bytes 8388624 | tf_op jit(solution)/shard_map/all_gather | solution.py:38
  204.6 30.3 %fusion.1 = f32[2048,256]{1,0:T(8,128)} fusion(bf16[2048,16384]{1,0:T(8,128)(2,1)} %multiply_convert_fusion, bf16[16384,256]{1,0:T(8,128)(2,1)} %all-gather.7.cloned.1.call-done), kind=kOutput, calls=%fused_computation.12 | convolution fusion | flops 17179869184 | bytes 77594624 | tf_op jit(solution)/shard_map/dot_general | solution.py:39
  234.8 0.0 reduce-scatter.7.cloned.1.call-update
  234.8 0.0 reduce-scatter.11.cloned.1.call-start
  234.9 0.0 all-gather.11.cloned.1.call-done
  234.9 30.3 %fusion.3 = f32[2048,256]{1,0:T(8,128)} fusion(bf16[2048,16384]{1,0:T(8,128)(2,1)} %multiply_convert_fusion, bf16[16384,256]{1,0:T(8,128)(2,1)} %all-gather.11.cloned.1.call-done), kind=kOutput, calls=%fused_computation.14 | convolution fusion | flops 17179869184 | bytes 77594624 | tf_op jit(solution)/shard_map/dot_general | solution.py:39
  265.3 0.0 all-gather.13.cloned.1.call-start
  265.3 0.1 reduce-scatter.7.cloned.1.call-done
  265.4 1.8 convert_element_type.65
  267.2 0.0 all-gather.17.cloned.1.call-start
  267.3 30.9 %reduce-scatter.11.cloned.1.call-done = f32[512,256]{1,0:T(8,128)} async-done(((f32[2048,256]{1,0:T(8,128)}), f32[512,256]{1,0:T(8,128)}) %reduce-scatter.11.cloned.1.call-update) | async-done | bytes 524304 | tf_op jit(solution)/shard_map/reduce_scatter | solution.py:40
  298.1 1.8 convert_element_type.68
  299.9 0.3 reduce-scatter.13.cloned.1.call-start
  300.2 21.0 %all-gather.13.cloned.1.call-done = bf16[2048,256]{1,0:T(8,128)(2,1)} async-done(((bf16[512,256]{1,0:T(8,128)(2,1)}), bf16[2048,256]{1,0:T(8,128)(2,1)}) %all-gather.13.cloned.1.call-update) | async-done | bytes 1048592 | tf_op jit(solution)/shard_map/all_gather | solution.py:41
  321.2 31.8 %fusion.4 = f32[16384,256]{1,0:T(8,128)} fusion(bf16[2048,16384]{1,0:T(8,128)(2,1)} %multiply_convert_fusion, bf16[2048,256]{1,0:T(8,128)(2,1)} %all-gather.13.cloned.1.call-done), kind=kOutput, calls=%fused_computation.15 | convolution fusion | flops 17179869184 | bytes 84934656 | tf_op jit(solution)/shard_map/dot_general | solution.py:42
  353.0 0.0 reduce-scatter.17.cloned.1.call-start
  353.1 0.0 all-gather.17.cloned.1.call-done
  353.1 31.9 %fusion.6 = f32[16384,256]{1,0:T(8,128)} fusion(bf16[2048,16384]{1,0:T(8,128)(2,1)} %multiply_convert_fusion, bf16[2048,256]{1,0:T(8,128)(2,1)} %all-gather.17.cloned.1.call-done), kind=kOutput, calls=%fused_computation.17 | convolution fusion | flops 17179869184 | bytes 84934656 | tf_op jit(solution)/shard_map/dot_general | solution.py:42
  385.0 0.0 all-gather.15.cloned.1.call-start
  385.1 0.0 reduce-scatter.13.cloned.1.call-done
  385.1 21.9 %reduce-scatter.17.cloned.1.call-done = f32[8192,256]{1,0:T(8,128)} async-done(((f32[16384,256]{1,0:T(8,128)}), f32[8192,256]{1,0:T(8,128)}) %reduce-scatter.17.cloned.1.call-update) | async-done | bytes 8388624 | tf_op jit(solution)/shard_map/reduce_scatter | solution.py:43
  407.0 14.0 %multiply_convert_fusion.1 = (bf16[8192,256]{1,0:T(8,128)(2,1)}, bf16[8192,256]{1,0:T(8,128)(2,1)}) fusion(bf16[8192,256]{1,0:T(8,128)(2,1)} %param.6, f32[8192,256]{1,0:T(8,128)} %reduce-scatter.17.cloned.1.call-done, f32[8192,256]{1,0:T(8,128)} %reduce-scatter.13.cloned.1.call-done, f32[8192,256]{1,0:T(8,128)} %reduce-scatter.9.cloned.1.call-done), kind=kLoop, calls=%fused_computation.2 | loop fusion | flops 25165824 | bytes 37748736 | tf_op jit(solution)/shard_map/convert_element_type | solution.py:49
  421.0 0.3 reduce-scatter.15.cloned.1.call-start
  421.3 19.0 %all-gather.15.cloned.1.call-done = bf16[16384,256]{1,0:T(8,128)(2,1)} async-done(((bf16[8192,256]{1,0:T(8,128)(2,1)}), bf16[16384,256]{1,0:T(8,128)(2,1)}) %all-gather.15.cloned.1.call-update) | async-done | bytes 8388624 | tf_op jit(solution)/shard_map/all_gather | solution.py:38
  440.3 30.3 %fusion.5 = f32[2048,256]{1,0:T(8,128)} fusion(bf16[2048,16384]{1,0:T(8,128)(2,1)} %multiply_convert_fusion, bf16[16384,256]{1,0:T(8,128)(2,1)} %all-gather.15.cloned.1.call-done), kind=kOutput, calls=%fused_computation.16 | convolution fusion | flops 17179869184 | bytes 77594624 | tf_op jit(solution)/shard_map/dot_general | solution.py:39
  470.6 0.0 all-reduce.5.cloned.1.call-start
  470.7 30.5 %reduce-scatter.15.cloned.1.call-done = f32[512,256]{1,0:T(8,128)} async-done(((f32[2048,256]{1,0:T(8,128)}), f32[512,256]{1,0:T(8,128)}) %reduce-scatter.15.cloned.1.call-update) | async-done | bytes 524304 | tf_op jit(solution)/shard_map/reduce_scatter | solution.py:40
  501.2 1.2 multiply_convert_fusion.2
  502.4 2.0 gather_fusion
  504.3 0.9 select_select_fusion
  505.3 42.7 %all-reduce.5.cloned.1.call-done = bf16[512,256]{1,0:T(8,128)(2,1)} async-done(((bf16[512,256]{1,0:T(8,128)(2,1)}), bf16[512,256]{1,0:T(8,128)(2,1)}) %all-reduce.5.cloned.1.call-update) | async-done | bytes 262160 | tf_op jit(solution)/shard_map/psum | solution.py:23
  548.0 10.8 %fusion.7 = f32[512,8192]{1,0:T(8,128)} fusion(bf16[512,256]{1,0:T(8,128)(2,1)} %all-reduce.5.cloned.1.call-done, bf16[8192,256]{1,0:T(8,128)(2,1)} %get-tuple-element.7), kind=kOutput, calls=%fused_computation.18 | convolution fusion | flops 2147483648 | bytes 21233664 | tf_op jit(solution)/shard_map/dot_general | solution.py:24
  (25 shorter events, 0.2 us)
Async XLA Ops:
  8.0 55.8 %all-reduce.3.cloned.1.call-start = ((), (), s32[]{:S(2)}) async-start(), calls=%async_computation.6 | async-start | bytes 131072 | tf_op jit(solution)/shard_map/psum | solution.py:11
  48.8 80.0 %all-gather.9.cloned.1.call-start = ((), (), s32[]{:S(2)}) async-start(), calls=%async_computation.9 | async-start | bytes 1310720 | tf_op jit(solution)/shard_map/all_gather | solution.py:41
  49.4 134.5 %reduce-scatter.9.cloned.1.call-start = ((), (), s32[]{:S(2)}) async-start(), calls=%async_computation.10 | async-start | bytes 25165824 | tf_op jit(solution)/shard_map/reduce_scatter | solution.py:43
  160.7 43.9 %all-gather.7.cloned.1.call-start = ((), (), s32[]{:S(2)}) async-start(), calls=%async_computation.7 | async-start | bytes 12582912 | tf_op jit(solution)/shard_map/all_gather | solution.py:38
  161.4 73.5 %all-gather.11.cloned.1.call-start = ((), (), s32[]{:S(2)}) async-start(), calls=%async_computation.11 | async-start | bytes 12582912 | tf_op jit(solution)/shard_map/all_gather | solution.py:38
  189.7 75.7 %reduce-scatter.7.cloned.1.call-start = ((), (), s32[]{:S(2)}) async-start(), calls=%async_computation.8 | async-start | bytes 2621440 | tf_op jit(solution)/shard_map/reduce_scatter | solution.py:40
  234.8 63.3 %reduce-scatter.11.cloned.1.call-start = ((), (), s32[]{:S(2)}) async-start(), calls=%async_computation.12 | async-start | bytes 2621440 | tf_op jit(solution)/shard_map/reduce_scatter | solution.py:40
  265.3 55.9 %all-gather.13.cloned.1.call-start = ((), (), s32[]{:S(2)}) async-start(), calls=%async_computation.13 | async-start | bytes 1310720 | tf_op jit(solution)/shard_map/all_gather | solution.py:41
  267.2 85.9 %all-gather.17.cloned.1.call-start = ((), (), s32[]{:S(2)}) async-start(), calls=%async_computation.17 | async-start | bytes 1310720 | tf_op jit(solution)/shard_map/all_gather | solution.py:41
  299.9 85.2 %reduce-scatter.13.cloned.1.call-start = ((), (), s32[]{:S(2)}) async-start(), calls=%async_computation.14 | async-start | bytes 25165824 | tf_op jit(solution)/shard_map/reduce_scatter | solution.py:43
  353.0 53.9 %reduce-scatter.17.cloned.1.call-start = ((), (), s32[]{:S(2)}) async-start(), calls=%async_computation.18 | async-start | bytes 25165824 | tf_op jit(solution)/shard_map/reduce_scatter | solution.py:43
  385.0 55.3 %all-gather.15.cloned.1.call-start = ((), (), s32[]{:S(2)}) async-start(), calls=%async_computation.15 | async-start | bytes 12582912 | tf_op jit(solution)/shard_map/all_gather | solution.py:38
  421.0 49.7 %copy-start.4 = (s32[512]{0:T(512)S(1)}, s32[512]{0:T(512)}, u32[]{:S(2)}) copy-start(s32[512]{0:T(512)} %param.7) | copy-start | bytes 6148
  421.0 80.2 %copy-start.1 = (f32[512,256]{1,0:T(8,128)S(1)}, f32[512,256]{1,0:T(8,128)}, u32[]{:S(2)}) copy-start(f32[512,256]{1,0:T(8,128)} %reduce-scatter.7.cloned.1.call-done) | copy-start | bytes 1572868
  421.0 80.2 %copy-start.2 = (f32[512,256]{1,0:T(8,128)S(1)}, f32[512,256]{1,0:T(8,128)}, u32[]{:S(2)}) copy-start(f32[512,256]{1,0:T(8,128)} %reduce-scatter.11.cloned.1.call-done) | copy-start | bytes 1572868
  421.0 80.2 %copy-start.3 = (bf16[512,256]{1,0:T(8,128)(2,1)S(1)}, bf16[512,256]{1,0:T(8,128)(2,1)}, u32[]{:S(2)}) copy-start(bf16[512,256]{1,0:T(8,128)(2,1)} %param.5) | copy-start | bytes 786436
  421.0 80.2 %reduce-scatter.15.cloned.1.call-start = ((), (), s32[]{:S(2)}) async-start(), calls=%async_computation.16 | async-start | bytes 2621440 | tf_op jit(solution)/shard_map/reduce_scatter | solution.py:40
  470.6 77.4 %all-reduce.5.cloned.1.call-start = ((), (), s32[]{:S(2)}) async-start(), calls=%async_computation.19 | async-start | bytes 524288 | tf_op jit(solution)/shard_map/psum | solution.py:23
  502.3 56.5 %copy-start = (bf16[512,256]{1,0:T(8,128)(2,1)}, bf16[512,256]{1,0:T(8,128)(2,1)S(1)}, u32[]{:S(2)}) copy-start(bf16[512,256]{1,0:T(8,128)(2,1)S(1)} %multiply_convert_fusion.2) | copy-start | bytes 786436
Sparse Core Ops, SparseCore 0:
  48.9 14.8 all-reduce.2
  160.8 23.0 reduce-scatter.8
  185.4 19.1 all-gather.6
  206.5 19.1 all-gather.10
  353.1 21.8 reduce-scatter.12
  385.1 21.7 reduce-scatter.16
  421.1 19.1 all-gather.14
Sparse Core Ops, SparseCore 1:
  51.1 23.4 all-gather.8
  234.9 30.4 reduce-scatter.6
  268.8 29.3 reduce-scatter.10
  300.5 20.6 all-gather.12
  323.5 20.6 all-gather.16
  470.7 30.4 reduce-scatter.14
  505.3 42.6 all-reduce.4
where the time goes:
time: 573 us; the launch traced here: 567 us
  waiting for transfers between devices  210 us (37%)
  matrix products  197 us (34%)
  other arithmetic  131 us (23%)
  between operations  16.2 us (3%)
  blocking collectives  9.35 us (2%)
    dot_general x3, matrix products, device_step(): lax.dot_general(norm_adj, user_panel, contract_rows, preferred_element_ty...  95.6 us
    dot_general x3, matrix products, device_step(): jnp.dot(norm_adj, item_panel, preferred_element_type=jnp.float32)  90.9 us
    convert_element_type x1, other arithmetic, norm_block(): (inv_user[:, None] * mask_blk.astype(jnp.float32) * inv_item[None, :]).as...  64.1 us
    reduce_scatter x3, waiting for transfers between devices, device_step(): lax.psum_scatter(user_part, 'col', scatter_dimension=0, tiled=True)  61.4 us
    reduce_scatter x3, waiting for transfers between devices, device_step(): lax.psum_scatter(item_part, 'row', scatter_dimension=0, tiled=True)  44.3 us
    psum x1, waiting for transfers between devices, query_scores(): picked = lax.psum(picked, ('row', 'col'))  42.7 us
    reduce_sum x1, other arithmetic, norm_block(): deg_user = lax.psum(jnp.sum(mask_blk, axis=1), 'col')  40.8 us
    all_gather x3, waiting for transfers between devices, device_step(): item_panel = lax.all_gather(item_cur, 'row', axis=0, tiled=True)  33.6 us
  transfers between devices with their start and end apart: 14, of which 10 were waited for; matrix products, arithmetic and copies ran while one was open for 35% of the time, Pallas kernels for 0%

commit v1 on v0

v1 whole, which is shorter than its diff:
```python
import functools

import jax
import jax.numpy as jnp
from jax import lax
from jax.experimental import pallas as pl
from jax.experimental.pallas import tpu as pltpu
from jax.sharding import PartitionSpec as P

LAYERS = 3
KT = 512
SLOTS = 10
SENDS = 4
VMEM_CAP = 60 * 1024 * 1024
MESH = pl.DeviceIdType.MESH
NN = (((1,), (0,)), ((), ()))
NT = (((1,), (1,)), ((), ()))


def pack_kernel(steps, mask_ref, bits_ref, rs_ref, cs_ref, row_acc):
    step = pl.program_id(0)
    rows, cols = mask_ref.shape

    @pl.when(step == 0)
    def _():
        row_acc[...] = jnp.zeros_like(row_acc)

    def block(b, col_acc):
        word = jnp.zeros((8, cols), jnp.int32)
        for j in range(32):
            at = pl.ds(pl.multiple_of(b * 256 + j * 8, 8), 8)
            m = mask_ref[at, :]
            word = word | lax.shift_left(m, j) if j else m
            col_acc = col_acc + m
            part = m[:, :128]
            for t in range(1, cols // 128):
                part = part + m[:, t * 128:(t + 1) * 128]
            row_acc[at, :] += part
        bits_ref[pl.ds(pl.multiple_of(b * 8, 8), 8), :] = word
        return col_acc

    col_acc = lax.fori_loop(0, rows // 256, block, jnp.zeros((8, cols), jnp.int32))
    cs_ref[...] = jnp.sum(col_acc, axis=0, keepdims=True)

    @pl.when(step == steps - 1)
    def _():
        for g in range(rows // 128):
            rs_ref[g:g + 1, :] = jnp.sum(row_acc[g * 128:(g + 1) * 128, :].T, axis=0, keepdims=True)


def pack(mask_blk):
    rows, cols = mask_blk.shape
    steps = cols // KT
    return pl.pallas_call(
        functools.partial(pack_kernel, steps),
        grid=(steps,),
        in_specs=[pl.BlockSpec((rows, KT), lambda i: (0, i))],
        out_specs=[pl.BlockSpec((rows // 32, KT), lambda i: (0, i)),
                   pl.BlockSpec((rows // 128, 128), lambda i: (0, 0)),
                   pl.BlockSpec((1, KT), lambda i: (0, i))],
        out_shape=[jax.ShapeDtypeStruct((rows // 32, cols), jnp.int32),
                   jax.ShapeDtypeStruct((rows // 128, 128), jnp.int32),
                   jax.ShapeDtypeStruct((1, cols), jnp.int32)],
        scratch_shapes=[pltpu.VMEM((rows, 128), jnp.int32)],
        compiler_params=pltpu.CompilerParams(dimension_semantics=('arbitrary',), vmem_limit_bytes=VMEM_CAP),
        name='pack',
    )(mask_blk)


def greet(peers):
    barrier = pltpu.get_barrier_semaphore()
    for dev in peers:
        pl.semaphore_signal(barrier, inc=1, device_id=dev, device_id_type=MESH)
    pl.semaphore_wait(barrier, len(peers))


def col_peer(col, row, n_col, off):
    return (lax.rem(col + off, n_col), row)


def degree_kernel(n_col, rs_ref, cs_ref, du_ref, di_ref, rs_in, cs_in, rs_send, rs_recv, cs_send, cs_recv):
    col, row = lax.axis_index('col'), lax.axis_index('row')
    other = (col, 1 - row)
    greet([other] + [col_peer(col, row, n_col, o) for o in range(1, n_col)])
    copies = [pltpu.make_async_remote_copy(src_ref=cs_ref, dst_ref=cs_in, send_sem=cs_send, recv_sem=cs_recv,
                                           device_id=other, device_id_type=MESH)]
    for o in range(1, n_col):
        copies.append(pltpu.make_async_remote_copy(
            src_ref=rs_ref, dst_ref=rs_in.at[o - 1], send_sem=rs_send.at[o - 1], recv_sem=rs_recv.at[o - 1],
            device_id=col_peer(col, row, n_col, o), device_id_type=MESH))
    for copy in copies:
        copy.start()
    for copy in copies:
        copy.wait()
    deg = rs_ref[...]
    for o in range(1, n_col):
        deg = deg + rs_in[o - 1]
    inv_user = lax.rsqrt(jnp.maximum(deg, 1).astype(jnp.float32))
    for g in range(inv_user.shape[0]):
        du_ref[g * 128:(g + 1) * 128, :] = jnp.broadcast_to(inv_user[g:g + 1, :], (128, 128)).T
    di_ref[...] = lax.rsqrt(jnp.maximum(cs_ref[...] + cs_in[...], 1).astype(jnp.float32))


def degrees(rs, cs, n_col):
    groups, cols = rs.shape[0], cs.shape[1]
    vmem = pl.BlockSpec(memory_space=pltpu.VMEM)
    return pl.pallas_call(
        functools.partial(degree_kernel, n_col),
        in_specs=[vmem, vmem],
        out_specs=[vmem, vmem],
        out_shape=[jax.ShapeDtypeStruct((groups * 128, 128), jnp.float32),
                   jax.ShapeDtypeStruct((1, cols), jnp.float32)],
        scratch_shapes=[pltpu.VMEM((n_col - 1,) + rs.shape, jnp.int32), pltpu.VMEM(cs.shape, jnp.int32),
                        pltpu.SemaphoreType.DMA((n_col - 1,)), pltpu.SemaphoreType.DMA((n_col - 1,)),
                        pltpu.SemaphoreType.DMA, pltpu.SemaphoreType.DMA],
        compiler_params=pltpu.CompilerParams(collective_id=0, has_side_effects=True),
        name='degrees',
    )(rs, cs)


def expand(bits_ref, du_ref, di, out_ref):
    cols = di.shape[1]

    def block(b, carry):
        word = bits_ref[pl.ds(pl.multiple_of(b * 8, 8), 8), :]
        for j in range(16):
            at = pl.multiple_of(b * 256 + j * 16, 16)
            halves = []
            for k in range(2):
                scale = du_ref[pl.ds(pl.multiple_of(at + k * 8, 8), 8), :]
                value = jnp.concatenate([scale] * (cols // 128), axis=1) * di
                hit = (word & (1 << (2 * j + k)) if 2 * j + k < 31 else word & (-2147483648)) != 0
                halves.append(jnp.where(hit, value, 0.0))
            out_ref[pl.ds(at, 16), :] = jnp.concatenate(halves, axis=0).astype(jnp.bfloat16)
        return carry

    lax.fori_loop(0, out_ref.shape[0] // 256, block, 0)


def adjacency_kernel(bits_ref, du_ref, di_ref, out_ref):
    expand(bits_ref, du_ref, jnp.broadcast_to(di_ref[...], (8, di_ref.shape[1])), out_ref.at[0])


def adjacency(bits, du, di):
    rows, cols = du.shape[0], bits.shape[1]
    steps = cols // KT
    return pl.pallas_call(
        adjacency_kernel,
        grid=(steps,),
        in_specs=[pl.BlockSpec((rows // 32, KT), lambda i: (0, i)),
                  pl.BlockSpec((rows, 128), lambda i: (0, 0)),
                  pl.BlockSpec((1, KT), lambda i: (0, i))],
        out_specs=pl.BlockSpec((1, rows, KT), lambda i: (i, 0, 0)),
        out_shape=jax.ShapeDtypeStruct((steps, rows, KT), jnp.bfloat16),
        compiler_params=pltpu.CompilerParams(dimension_semantics=('arbitrary',), vmem_limit_bytes=VMEM_CAP),
        name='adjacency',
    )(bits, du, di)


def layer_kernel(n_col, adj, item_own, user_own, item_next, user_next,
                 abuf, panel, acc, upan, ut, rs_in, ix_in, ix_out,
                 a_sem, own_sem, pan_send, pan_recv, uown_sem, u_send, u_recv, rs_send, rs_recv, ix_send, ix_recv):
    col, row = lax.axis_index('col'), lax.axis_index('row')
    other = (col, 1 - row)
    chunks = adj.shape[0]
    half = chunks // 2
    slots = abuf.shape[0]
    sends = ix_out.shape[0]
    own_rows = acc.shape[0] // n_col

    def user_chunk(t):
        return jnp.where(t < half, row * half + t, (1 - row) * half + t - half)

    def turn(q):
        return lax.rem(q + half - slots + half, half)

    def item_chunk(q):
        return jnp.where(q < half, (1 - row) * half + turn(q), row * half + turn(q - half))

    def load(chunk, slot):
        return pltpu.make_async_copy(adj.at[chunk], abuf.at[slot], a_sem.at[slot])

    greet([other] + [col_peer(col, row, n_col, o) for o in range(1, n_col)])

    own_copy = pltpu.make_async_copy(item_own, panel.at[0], own_sem)
    own_copy.start()
    pan_copy = pltpu.make_async_remote_copy(src_ref=item_own, dst_ref=panel.at[1], send_sem=pan_send,
                                            recv_sem=pan_recv, device_id=other, device_id_type=MESH)
    pan_copy.start()
    for t in range(slots - 1):
        load(user_chunk(t), t).start()
    uown_copy = pltpu.make_async_copy(user_own, upan.at[col], uown_sem)
    uown_copy.start()
    u_copies = [pltpu.make_async_remote_copy(
        src_ref=user_own, dst_ref=upan.at[col], send_sem=u_send.at[o - 1], recv_sem=u_recv.at[o - 1],
        device_id=col_peer(col, row, n_col, o), device_id_type=MESH) for o in range(1, n_col)]
    for copy in u_copies:
        copy.start()
    acc[...] = jnp.zeros_like(acc)
    own_copy.wait()

    def user_step(side, t, carry):
        slot = lax.rem(t, slots)

        @pl.when(t + slots - 1 < chunks)
        def _():
            load(user_chunk(t + slots - 1), lax.rem(t + slots - 1, slots)).start()

        load(user_chunk(t), slot).wait()
        at = pl.ds(pl.multiple_of((t - side * half) * KT, KT), KT)
        acc[...] += lax.dot_general(abuf[slot], panel[side, at, :], NN, preferred_element_type=jnp.float32)
        return carry

    lax.fori_loop(0, half, functools.partial(user_step, 0), 0)
    pan_copy.wait()
    lax.fori_loop(half, chunks, functools.partial(user_step, 1), 0)

    uown_copy.wait()
    for copy in u_copies:
        copy.wait()
    for c in range(n_col):
        ut[:, c * own_rows:(c + 1) * own_rows] = upan[c].T

    rs_copies = []
    for o in range(1, n_col):
        dest = lax.rem(col + o, n_col)
        rs_copies.append(pltpu.make_async_remote_copy(
            src_ref=acc.at[pl.ds(pl.multiple_of(dest * own_rows, own_rows), own_rows), :], dst_ref=rs_in.at[o - 1],
            send_sem=rs_send.at[o - 1], recv_sem=rs_recv.at[o - 1],
            device_id=(dest, row), device_id_type=MESH))
    for copy in rs_copies:
        copy.start()

    def ix_copy(q):
        return pltpu.make_async_remote_copy(
            src_ref=ix_out.at[lax.rem(q, sends)], dst_ref=ix_in.at[turn(q)], send_sem=ix_send.at[lax.rem(q, sends)],
            recv_sem=ix_recv.at[turn(q)], device_id=other, device_id_type=MESH)

    def product(q):
        slot = lax.rem(chunks + q, slots)

        @pl.when((q >= 1) & (q - 1 + slots < chunks))
        def _():
            load(item_chunk(q - 1 + slots), lax.rem(chunks + q - 1, slots)).start()

        @pl.when(q >= slots)
        def _():
            load(item_chunk(q), slot).wait()

        return lax.dot_general(ut[...], abuf[slot], NN, preferred_element_type=jnp.float32)

    def give_step(q, carry):
        part = product(q)

        @pl.when(q >= sends)
        def _():
            ix_copy(q - sends).wait_send()

        ix_out[lax.rem(q, sends)] = part
        ix_copy(q).start()
        return carry

    lax.fori_loop(0, half, give_step, 0)

    def keep_step(q, carry):
        part = product(q)
        j = turn(q - half)
        ix_copy(q - half).wait_recv()
        whole = (part + ix_in[j]).astype(jnp.bfloat16)
        item_next[pl.ds(pl.multiple_of(j * KT, KT), KT), :] = whole.T
        return carry

    lax.fori_loop(half, chunks, keep_step, 0)

    for q in range(half - sends, half):
        ix_copy(q).wait_send()
    for copy in rs_copies:
        copy.wait()
    total = acc[pl.ds(pl.multiple_of(col * own_rows, own_rows), own_rows), :]
    for o in range(1, n_col):
        total = total + rs_in[o - 1]
    user_next[...] = total.astype(jnp.bfloat16)


def layer(adj, item_own, user_own, n_col):
    chunks, rows, _ = adj.shape
    items, emb = item_own.shape
    users = user_own.shape[0]
    half = chunks // 2
    anyspace = pl.BlockSpec(memory_space=pl.ANY)
    vmem = pl.BlockSpec(memory_space=pltpu.VMEM)
    dma = pltpu.SemaphoreType.DMA
    flops = 4 * chunks * rows * KT * emb
    return pl.pallas_call(
        functools.partial(layer_kernel, n_col),
        in_specs=[anyspace, anyspace, anyspace],
        out_specs=[vmem, vmem],
        out_shape=[jax.ShapeDtypeStruct((items, emb), jnp.bfloat16),
                   jax.ShapeDtypeStruct((users, emb), jnp.bfloat16)],
        scratch_shapes=[
            pltpu.VMEM((SLOTS, rows, KT), jnp.bfloat16),
            pltpu.VMEM((2, items, emb), jnp.bfloat16),
            pltpu.VMEM((rows, emb), jnp.float32),
            pltpu.VMEM((n_col, users, emb), jnp.bfloat16),
            pltpu.VMEM((emb, rows), jnp.bfloat16),
            pltpu.VMEM((n_col - 1, users, emb), jnp.float32),
            pltpu.VMEM((half, emb, KT), jnp.float32),
            pltpu.VMEM((SENDS, emb, KT), jnp.float32),
            dma((SLOTS,)), dma, dma, dma, dma,
            dma((n_col - 1,)), dma((n_col - 1,)), dma((n_col - 1,)), dma((n_col - 1,)),
            dma((SENDS,)), dma((half,)),
        ],
        cost_estimate=pl.CostEstimate(flops=flops, bytes_accessed=adj.size * 4, transcendentals=0),
        compiler_params=pltpu.CompilerParams(collective_id=1, has_side_effects=True, vmem_limit_bytes=VMEM_CAP),
        name='layer',
    )(adj, item_own, user_own)


def pick_kernel(n_col, u0, u1, u2, u3, query, final_user, picked, mine, parts, one_send, one_recv, two_send, two_recv):
    col, row = lax.axis_index('col'), lax.axis_index('row')
    n_dev = 2 * n_col
    me = col * 2 + row
    share = picked.shape[0] // n_dev
    rows = u0.shape[0]

    def dev(o):
        lin = lax.rem(me + o, n_dev)
        return lin, (lin // 2, lin % 2)

    greet([dev(o)[1] for o in range(1, n_dev)])
    total = u0[...].astype(jnp.float32) + u1[...].astype(jnp.float32)
    total = total + u2[...].astype(jnp.float32)
    total = total + u3[...].astype(jnp.float32)
    final = (total / (LAYERS + 1)).astype(jnp.bfloat16)
    final_user[...] = final
    local = query[...] - (row * n_col + col) * rows
    hot = lax.broadcasted_iota(jnp.int32, (query.shape[0], rows), 1) == local
    mine[...] = jnp.dot(hot.astype(jnp.bfloat16), final, preferred_element_type=jnp.float32).astype(jnp.bfloat16)

    def rows_of(lin):
        return pl.ds(pl.multiple_of(lin * share, share), share)

    first = []
    for o in range(1, n_dev):
        lin, dest = dev(o)
        first.append(pltpu.make_async_remote_copy(
            src_ref=mine.at[rows_of(lin), :], dst_ref=parts.at[o - 1], send_sem=one_send.at[o - 1],
            recv_sem=one_recv.at[o - 1], device_id=dest, device_id_type=MESH))
    for copy in first:
        copy.start()
    for copy in first:
        copy.wait()
    found = mine[rows_of(me), :].astype(jnp.float32)
    for o in range(1, n_dev):
        found = found + parts[o - 1].astype(jnp.float32)
    picked[rows_of(me), :] = found.astype(jnp.bfloat16)
    second = []
    for o in range(1, n_dev):
        second.append(pltpu.make_async_remote_copy(
            src_ref=picked.at[rows_of(me), :], dst_ref=picked.at[rows_of(me), :], send_sem=two_send.at[o - 1],
            recv_sem=two_recv.at[o - 1], device_id=dev(o)[1], device_id_type=MESH))
    for copy in second:
        copy.start()
    for copy in second:
        copy.wait()


def pick(users, queries, n_col):
    n_dev = 2 * n_col
    rows, emb = users[0].shape
    n_query = queries.shape[0]
    vmem = pl.BlockSpec(memory_space=pltpu.VMEM)
    dma = pltpu.SemaphoreType.DMA
    return pl.pallas_call(
        functools.partial(pick_kernel, n_col),
        in_specs=[vmem] * 5,
        out_specs=[vmem, vmem],
        out_shape=[jax.ShapeDtypeStruct((rows, emb), jnp.bfloat16),
                   jax.ShapeDtypeStruct((n_query, emb), jnp.bfloat16)],
        scratch_shapes=[pltpu.VMEM((n_query, emb), jnp.bfloat16),
                        pltpu.VMEM((n_dev - 1, n_query // n_dev, emb), jnp.bfloat16),
                        dma((n_dev - 1,)), dma((n_dev - 1,)), dma((n_dev - 1,)), dma((n_dev - 1,))],
        compiler_params=pltpu.CompilerParams(collective_id=2, has_side_effects=True),
        name='pick',
    )(*users, queries[:, None])


def score_kernel(i0, i1, i2, i3, picked, final_item, scores):
    total = i0[...].astype(jnp.float32) + i1[...].astype(jnp.float32)
    total = total + i2[...].astype(jnp.float32)
    total = total + i3[...].astype(jnp.float32)
    final = (total / (LAYERS + 1)).astype(jnp.bfloat16)
    final_item[...] = final
    scores[...] = lax.dot_general(picked[...], final, NT, preferred_element_type=jnp.float32)


def score(items, picked):
    rows, emb = items[0].shape
    n_query = picked.shape[0]
    tile = 1024
    block = pl.BlockSpec((tile, emb), lambda i: (i, 0))
    return pl.pallas_call(
        score_kernel,
        grid=(rows // tile,),
        in_specs=[block] * 4 + [pl.BlockSpec((n_query, emb), lambda i: (0, 0))],
        out_specs=[block, pl.BlockSpec((n_query, tile), lambda i: (0, i))],
        out_shape=[jax.ShapeDtypeStruct((rows, emb), jnp.bfloat16),
                   jax.ShapeDtypeStruct((n_query, rows), jnp.float32)],
        compiler_params=pltpu.CompilerParams(dimension_semantics=('arbitrary',), vmem_limit_bytes=VMEM_CAP),
        name='score',
    )(*items, picked)


def solution(mesh):
    n_col = mesh.shape['col']

    def device_step(mask_blk, user_shard, item_shard, queries):
        bits, rs, cs = pack(mask_blk)
        du, di = degrees(rs, cs, n_col)
        adj = adjacency(bits, du, di)
        users, items = [user_shard], [item_shard]
        for _ in range(LAYERS):
            item_next, user_next = layer(adj, items[-1], users[-1], n_col)
            users.append(user_next)
            items.append(item_next)
        final_user, picked = pick(users, queries, n_col)
        final_item, scores = score(items, picked)
        return final_user, final_item, scores

    return jax.shard_map(device_step, mesh=mesh, in_specs=(P('row', 'col'), P(('row', 'col'), None), P(('col', 'row'), None), P()), out_specs=(P(('row', 'col'), None), P(('col', 'row'), None), P(None, ('col', 'row'))), check_vma=False)
```

time: 573 us -> 303 us (0.53)
  Pallas kernels: 0 us -> 299 us
  waiting for transfers between devices: 210 us -> 0 us
  matrix products: 197 us -> 0 us
  other arithmetic: 131 us -> 0 us
  between operations: 16.2 us -> 0.7 us
  blocking collectives: 9.35 us -> 0 us
    pallas_call x0 -> x8, Pallas kernels: none -> 299 us  [the longest x3 175 us: layer(): pl.pallas_call(functools.partial(layer_kernel, n_col), in_specs=[anyspace...]
    dot_general x7 -> x0, matrix products: 197 us -> none  [the longest x3 95.6 us: device_step(): lax.dot_general(norm_adj, user_panel, contract_rows, preferred_element_ty...]
    reduce_scatter x6 -> x0, waiting for transfers between devices: 106 us -> none  [the longest x3 61.4 us: device_step(): lax.psum_scatter(user_part, 'col', scatter_dimension=0, tiled=True)]
    convert_element_type x6 -> x0, other arithmetic: 88.6 us -> none  [the longest x1 64.1 us: norm_block(): (inv_user[:, None] * mask_blk.astype(jnp.float32) * inv_item[None, :]).as...]
    all_gather x6 -> x0, waiting for transfers between devices: 54.6 us -> none  [the longest x3 33.6 us: device_step(): item_panel = lax.all_gather(item_cur, 'row', axis=0, tiled=True)]
    psum x2 -> x0, waiting for transfers between devices: 47.8 us -> none  [the longest x1 42.7 us: query_scores(): picked = lax.psum(picked, ('row', 'col'))]
    reduce_sum x1 -> x0, other arithmetic: 40.8 us -> none  [norm_block(): deg_user = lax.psum(jnp.sum(mask_blk, axis=1), 'col')]
    psum x1 -> x0, blocking collectives: 9.35 us -> none  [norm_block(): deg_user = lax.psum(jnp.sum(mask_blk, axis=1), 'col')]
  transfers between devices with their start and end apart: 14 -> 0, of which waited for: 10 -> 0; matrix products, arithmetic and copies ran while one was open for 35% -> 0% of each run, Pallas kernels for 0% -> 0%
where the time goes in v1:
time: 303 us; the launch traced here: 301 us
  Pallas kernels  299 us (99%)
    pallas_call x3, Pallas kernels, layer(): pl.pallas_call(functools.partial(layer_kernel, n_col), in_specs=[anyspace...  175 us
    pallas_call x1, Pallas kernels, pack(): pl.pallas_call(functools.partial(pack_kernel, steps), grid=(steps,), in_s...  51.3 us
    pallas_call x1, Pallas kernels, adjacency(): pl.pallas_call(adjacency_kernel, grid=(steps,), in_specs=[pl.BlockSpec((r...  34.6 us
    pallas_call x1, Pallas kernels, score(): pl.pallas_call(score_kernel, grid=(rows // tile,), in_specs=[block] * 4 +...  15.9 us
    pallas_call x1, Pallas kernels, pick(): pl.pallas_call(functools.partial(pick_kernel, n_col), in_specs=[vmem] * 5...  13.3 us
    pallas_call x1, Pallas kernels, degrees(): pl.pallas_call(functools.partial(degree_kernel, n_col), in_specs=[vmem, v...  8.81 us

profile of v1, /device:TPU:0, one launch (start us, length us, event | category | flops | bytes accessed | tf_op | source)
XLA Modules:
  0.0 301.0 jit_solution(3448491524876549079)
XLA Ops:
  0.6 51.3 %pack.1 = (s32[64,16384]{1,0:T(8,128)}, s32[16,128]{1,0:T(8,128)}, s32[1,16384]{1,0:T(1,128)}) custom-call(s32[2048,16384]{1,0:T(8,128)} %mask_ref.1), custom_call_target="tpu_custom_call" | custom-call | tf_op jit(solution)/shard_map/pack/pallas_call | solution.py:54
  51.9 8.8 %degrees.1 = (f32[2048,128]{1,0:T(8,128)}, f32[1,16384]{1,0:T(1,128)}) custom-call(s32[16,128]{1,0:T(8,128)} %get-tuple-element.19.rs_ref, s32[1,16384]{1,0:T(1,128)} %get-tuple-element.20.cs_ref), custom_call_target="tpu_custom_call" | custom-call | tf_op jit(solution)/shard_map/degrees/pallas_call | solution.py:107
  60.7 34.6 %adjacency.1.adj = bf16[32,2048,512]{2,1,0:T(8,128)(2,1)} custom-call(s32[64,16384]{1,0:T(8,128)} %get-tuple-element.18.bits_ref, f32[2048,128]{1,0:T(8,128)} %get-tuple-element.21.du_ref, f32[1,16384]{1,0:T(1,128)} %get-tuple-element.22.di_ref), custom_call_target="tpu_custom_call" | custom-call | tf_op jit(solution)/shard_map/adjacency/pallas_call | solution.py:147
  95.3 58.8 %layer.3 = (bf16[8192,256]{1,0:T(8,128)(2,1)}, bf16[512,256]{1,0:T(8,128)(2,1)}) custom-call(bf16[32,2048,512]{2,1,0:T(8,128)(2,1)} %adjacency.1.adj, bf16[8192,256]{1,0:T(8,128)(2,1)} %i0.1, bf16[512,256]{1,0:T(8,128)(2,1)} %u0.1), custom_call_target="tpu_custom_call" | custom-call | flops 34359738368 | bytes 134217728 | tf_op jit(solution)/shard_map/layer/pallas_call | solution.py:294
  154.2 57.0 %layer.4 = (bf16[8192,256]{1,0:T(8,128)(2,1)}, bf16[512,256]{1,0:T(8,128)(2,1)}) custom-call(bf16[32,2048,512]{2,1,0:T(8,128)(2,1)} %adjacency.1.adj, bf16[8192,256]{1,0:T(8,128)(2,1)} %get-tuple-element.24.item_own.i1, bf16[512,256]{1,0:T(8,128)(2,1)} %get-tuple-element.23.user_own.u1), custom_call_target="tpu_custom_call" | custom-call | flops 34359738368 | bytes 134217728 | tf_op jit(solution)/shard_map/layer/pallas_call | solution.py:294
  211.2 0.0 copy-start.1
  211.2 59.0 %layer.5 = (bf16[8192,256]{1,0:T(8,128)(2,1)}, bf16[512,256]{1,0:T(8,128)(2,1)}) custom-call(bf16[32,2048,512]{2,1,0:T(8,128)(2,1)} %adjacency.1.adj, bf16[8192,256]{1,0:T(8,128)(2,1)} %get-tuple-element.26.item_own.i2, bf16[512,256]{1,0:T(8,128)(2,1)} %get-tuple-element.25.user_own.u2), custom_call_target="tpu_custom_call" | custom-call | flops 34359738368 | bytes 134217728 | tf_op jit(solution)/shard_map/layer/pallas_call | solution.py:294
  270.2 0.0 copy-done.1
  270.2 0.9 copy.7.query
  271.1 13.3 %pick.1 = (bf16[512,256]{1,0:T(8,128)(2,1)}, bf16[512,256]{1,0:T(8,128)(2,1)}) custom-call(bf16[512,256]{1,0:T(8,128)(2,1)} %u0.1, bf16[512,256]{1,0:T(8,128)(2,1)} %get-tuple-element.23.user_own.u1, bf16[512,256]{1,0:T(8,128)(2,1)} %get-tuple-element.25.user_own.u2, bf16[512,256]{1,0:T(8,128)(2,1)} %get-tuple-element.27.u3, s32[512,1]{1,0:T(8,128)} %copy.7.query), custom_call_target="tpu_custom_call" | custom-call | tf_op jit(solution)/shard_map/pick/pallas_call | solution.py:374
  284.4 0.0 copy-start
  284.4 15.9 %score.1 = (bf16[8192,256]{1,0:T(8,128)(2,1)}, f32[512,8192]{1,0:T(8,128)}) custom-call(bf16[8192,256]{1,0:T(8,128)(2,1)} %i0.1, bf16[8192,256]{1,0:T(8,128)(2,1)} %get-tuple-element.24.item_own.i1, bf16[8192,256]{1,0:T(8,128)(2,1)} %get-tuple-element.26.item_own.i2, bf16[8192,256]{1,0:T(8,128)(2,1)} %get-tuple-element.29.i3, ...), custom_call_target="tpu_custom_call" | custom-call | tf_op jit(solution)/shard_map/score/pallas_call | solution.py:402
  300.3 0.0 copy-done
  300.3 0.7 copy.9
Async XLA Ops:
  211.2 59.0 %copy-start.1 = (s32[512]{0:T(512)S(1)}, s32[512]{0:T(512)}, u32[]{:S(2)}) copy-start(s32[512]{0:T(512)} %param.7) | copy-start | bytes 6148
  284.4 15.9 %copy-start = (bf16[512,256]{1,0:T(8,128)(2,1)S(1)}, bf16[512,256]{1,0:T(8,128)(2,1)}, u32[]{:S(2)}) copy-start(bf16[512,256]{1,0:T(8,128)(2,1)} %get-tuple-element.36) | copy-start | bytes 786436

commit v2 on v0

v2 whole, which is shorter than its diff:
```python
import functools

import jax
import jax.numpy as jnp
from jax import lax
from jax.experimental import pallas as pl
from jax.experimental.pallas import tpu as pltpu
from jax.sharding import PartitionSpec as P

LAYERS = 3
KT = 512
GROUP = 4
ROWS = 1024
RING = 4
VMEM_CAP = 67043328
MESH = pl.DeviceIdType.MESH
NT = (((1,), (1,)), ((), ()))


def pack_kernel(mask, bits, rs_ref, cs_ref, buf, out, row_acc, in_sem, out_sem):
    rows, cols = mask.shape
    steps = cols // KT

    def columns(i):
        return pl.ds(pl.multiple_of(i * KT, KT), KT)

    def load(i):
        slot = lax.rem(i, RING)
        return pltpu.make_async_copy(mask.at[:, columns(i)], buf.at[slot], in_sem.at[slot])

    def save(i):
        slot = lax.rem(i, 2)
        return pltpu.make_async_copy(out.at[slot], bits.at[:, columns(i)], out_sem.at[slot])

    for i in range(RING - 1):
        load(i).start()
    row_acc[...] = jnp.zeros_like(row_acc)

    def step(i, carry):
        slot = lax.rem(i, RING)

        @pl.when(i + RING - 1 < steps)
        def _():
            load(i + RING - 1).start()

        @pl.when(i >= 2)
        def _():
            save(i - 2).wait()

        load(i).wait()

        def block(b, col_acc):
            words = []
            for k in range(2):
                word = jnp.zeros((8, KT), jnp.int32)
                for j in range(16):
                    at = pl.ds(pl.multiple_of(b * 256 + j * 16 + k * 8, 8), 8)
                    m = buf[slot, at, :]
                    word = word | (lax.shift_left(m, j) if j else m)
                    col_acc = col_acc + m
                    part = m[:, :128]
                    for t in range(1, KT // 128):
                        part = part + m[:, t * 128:(t + 1) * 128]
                    row_acc[at, :] += part
                words.append(word)
            out[lax.rem(i, 2), pl.ds(pl.multiple_of(b * 16, 16), 16), :] = jnp.concatenate(words, axis=0).astype(jnp.int16)
            return col_acc

        col_acc = lax.fori_loop(0, rows // 256, block, jnp.zeros((8, KT), jnp.int32))
        cs_ref[:, columns(i)] = jnp.sum(col_acc, axis=0, keepdims=True)
        save(i).start()
        return carry

    lax.fori_loop(0, steps, step, 0)
    for g in range(rows // 128):
        rs_ref[g:g + 1, :] = jnp.sum(row_acc[g * 128:(g + 1) * 128, :].T, axis=0, keepdims=True)
    save(steps - 2).wait()
    save(steps - 1).wait()


def pack(mask_blk):
    rows, cols = mask_blk.shape
    vmem = pl.BlockSpec(memory_space=pltpu.VMEM)
    anyspace = pl.BlockSpec(memory_space=pl.ANY)
    return pl.pallas_call(
        pack_kernel,
        in_specs=[anyspace],
        out_specs=[anyspace, vmem, vmem],
        out_shape=[jax.ShapeDtypeStruct((rows // 16, cols), jnp.int16),
                   jax.ShapeDtypeStruct((rows // 128, 128), jnp.int32),
                   jax.ShapeDtypeStruct((1, cols), jnp.int32)],
        scratch_shapes=[pltpu.VMEM((RING, rows, KT), jnp.int32), pltpu.VMEM((2, rows // 16, KT), jnp.int16),
                        pltpu.VMEM((rows, 128), jnp.int32),
                        pltpu.SemaphoreType.DMA((RING,)), pltpu.SemaphoreType.DMA((2,))],
        compiler_params=pltpu.CompilerParams(vmem_limit_bytes=VMEM_CAP),
        name='pack',
    )(mask_blk)


def greet(peers):
    barrier = pltpu.get_barrier_semaphore()
    for dev in peers:
        pl.semaphore_signal(barrier, inc=1, device_id=dev, device_id_type=MESH)
    pl.semaphore_wait(barrier, len(peers))


def expand(bits, du, di, out):
    cols = out.shape[1]
    wide = jnp.broadcast_to(di, (16, cols))
    zero = jnp.zeros((16, cols), jnp.bfloat16)
    for b in range(out.shape[0] // 256):
        word = bits[b * 16:(b + 1) * 16, :]
        for j in range(16):
            at = b * 256 + j * 16
            value = jnp.concatenate([du[at:at + 16, :]] * (cols // 128), axis=1) * wide
            hit = (word & jnp.int16(1 << j if j < 15 else -32768)) != 0
            out[at:at + 16, :] = jnp.where(hit, value.astype(jnp.bfloat16), zero)


def spread_kernel(n_col, bits, rs_ref, cs_ref, item0, user0, query, adj, final_item, final_user, picked,
                  abuf, bwin, panel, stash, acc, upan, ut, unew, user_sum, di, rs_in, ix_in, ix_out, mine, parts,
                  deg_in, cnt_in,
                  a_sem, st_sem, b_sem, own_sem, uown_sem, f_sem, deg_send, deg_recv, cnt_send, cnt_recv,
                  p_send, p_recv, u_send, u_recv, r_send, r_recv, x_send, x_recv, one_send, one_recv, two_send, two_recv):
    col, row = lax.axis_index('col'), lax.axis_index('row')
    other = (col, 1 - row)
    n_dev = 2 * n_col
    chunks = adj.shape[0]
    half = chunks // 2
    groups = half // GROUP
    steps = 2 * groups
    rows, emb = acc.shape[1], acc.shape[2]
    wide = GROUP * KT
    own_items = half * KT
    own_rows = rows // n_col
    sides = [(lax.rem(col + o, n_col), row) for o in range(1, n_col)]
    me = col * 2 + row

    def device(o):
        lin = lax.rem(me + o, n_dev)
        return lin, (lin // 2, lin % 2)

    def remote(src, dst, send, recv, dest):
        return pltpu.make_async_remote_copy(src_ref=src, dst_ref=dst, send_sem=send, recv_sem=recv,
                                            device_id=dest, device_id_type=MESH)

    greet([device(o)[1] for o in range(1, n_dev)])

    counts = [remote(cs_ref, cnt_in, cnt_send, cnt_recv, other)]
    counts += [remote(rs_ref, deg_in.at[i], deg_send.at[i], deg_recv.at[i], sides[i]) for i in range(n_col - 1)]
    for copy in counts:
        copy.start()

    def turn(phase, pos):
        return lax.rem(phase + pos, groups)

    def item_rows(side, g):
        return pl.ds(pl.multiple_of(side * own_items + g * wide, wide), wide)

    def give_panel(g):
        return remote(panel.at[item_rows(0, g), :], panel.at[item_rows(1, g), :], p_send.at[g], p_recv.at[g], other)

    def first_panel(g):
        return remote(item0.at[item_rows(0, g), :], panel.at[item_rows(1, g), :], p_send.at[g], p_recv.at[g], other)

    def own_panel(side):
        return pltpu.make_async_copy(item0, panel.at[pl.ds(side * own_items, own_items), :], own_sem)

    def chunk_of(near, g):
        return jnp.where(near, row, 1 - row) * half + g * GROUP

    def bits_copy(u, slot):
        at = chunk_of(u < groups, lax.rem(u, groups)) * KT
        return pltpu.make_async_copy(bits.at[:, pl.ds(pl.multiple_of(at, wide), wide)], bwin.at[slot], b_sem.at[slot])

    def adj_group(chunk):
        return adj.at[pl.ds(chunk, GROUP)]

    def ring_group(slot):
        return abuf.at[pl.ds(slot * GROUP, GROUP)]

    bits_copy(0, 0).start()
    bits_copy(1, 1).start()
    own_panel(0).start()
    for g in range(groups):
        first_panel(g).start()

    def user_sends(src):
        return [remote(src, upan.at[col], u_send.at[i], u_recv.at[i], sides[i]) for i in range(n_col - 1)]

    for copy in user_sends(user0):
        copy.start()
    upan[col] = user0[...]
    user_sum[...] = user0[...].astype(jnp.float32)
    acc[0] = jnp.zeros(acc.shape[1:], acc.dtype)

    for copy in counts:
        copy.wait()
    degree = rs_ref[...]
    for i in range(n_col - 1):
        degree = degree + deg_in[i]
    inv_user = lax.rsqrt(jnp.maximum(degree, 1).astype(jnp.float32))
    du = acc.at[1, :, pl.ds(0, 128)]
    for g in range(rows // 128):
        du[g * 128:(g + 1) * 128, :] = jnp.broadcast_to(inv_user[g:g + 1, :], (128, 128)).T
    di[...] = lax.rsqrt(jnp.maximum(cs_ref[...] + cnt_in[...], 1).astype(jnp.float32))

    def make_group(u, slot, base):
        at = chunk_of(u < groups, lax.rem(u, groups)) * KT
        for k in range(GROUP):
            scale = di[:, pl.ds(pl.multiple_of(at + k * KT, KT), KT)]
            expand(bwin.at[slot, :, pl.ds(k * KT, KT)], du, scale, abuf.at[base + k])

    def user_product(layer, base, where):
        table = panel[where, :]
        for m in range(0, rows, ROWS):
            m_rows = pl.ds(m, ROWS)
            left = jnp.concatenate([abuf[base + k, m_rows, :] for k in range(GROUP)], axis=1)
            acc[layer % 2, m_rows, :] += jnp.dot(left, table, preferred_element_type=jnp.float32)

    def save(u, slot):
        return pltpu.make_async_copy(ring_group(slot), adj_group(chunk_of(u < groups, lax.rem(u, groups))), st_sem.at[slot])

    def fetch(chunk, slot):
        return pltpu.make_async_copy(adj_group(chunk), ring_group(slot), a_sem.at[slot])

    bits_copy(0, 0).wait()
    make_group(0, 0, 0)
    save(0, 0).start()
    own_panel(0).wait()
    last = groups - 1

    def first_step(i, carry):
        @pl.when(i > 0)
        def _():
            save(2 * i - 1, 1).wait()

        @pl.when(2 * i == groups)
        def _():
            for g in range(groups):
                first_panel(g).wait()

        @pl.when(i == last)
        def _():
            fetch(chunk_of(False, groups - 3), 2).start()

        again = jnp.where(i < last, 2 * i + 2, 2 * i)
        bits_copy(again, 0).start()
        bits_copy(2 * i + 1, 1).wait()
        make_group(2 * i + 1, 1, GROUP)
        user_product(0, 0, pl.ds(pl.multiple_of(2 * i * wide, wide), wide))
        save(2 * i + 1, 1).start()
        save(2 * i, 0).wait()

        @pl.when(i < last)
        def _():
            bits_copy(2 * i + 3, 1).start()

        bits_copy(again, 0).wait()
        make_group(again, 0, 0)
        user_product(0, GROUP, pl.ds(pl.multiple_of((2 * i + 1) * wide, wide), wide))

        @pl.when(i < last)
        def _():
            save(2 * i + 2, 0).start()

        return carry

    lax.fori_loop(0, groups, first_step, 0)
    save(steps - 1, 1).wait()

    def ring_slot(phase, pos):
        return lax.rem(5 * phase + pos, 3)

    def phase_chunk(phase, pos):
        users_first = phase % 2 == 0
        near = pos < groups if users_first else pos >= groups
        return chunk_of(near, turn(phase, pos))

    def stream(phase, pos):
        @pl.when((pos >= 1) & (pos + 2 < steps))
        def _():
            fetch(phase_chunk(phase, pos + 2), ring_slot(phase, pos + 2)).start()

        if phase == 1:
            @pl.when(pos == 0)
            def _():
                fetch(phase_chunk(phase, 0), ring_slot(phase, 0)).wait()

        @pl.when(pos >= 3)
        def _():
            fetch(phase_chunk(phase, pos), ring_slot(phase, pos)).wait()

        return ring_slot(phase, pos) * GROUP

    def shares(layer):
        out = []
        for i in range(n_col - 1):
            at = pl.multiple_of(sides[i][0] * own_rows, own_rows)
            out.append(remote(acc.at[layer % 2, pl.ds(at, own_rows), :], rs_in.at[i], r_send.at[i], r_recv.at[i], sides[i]))
        return out

    def user_rows(layer):
        for copy in shares(layer):
            copy.wait()
        total = acc[layer % 2, pl.ds(pl.multiple_of(col * own_rows, own_rows), own_rows), :]
        for i in range(n_col - 1):
            total = total + rs_in[i]
        fresh = total.astype(jnp.bfloat16)
        user_sum[...] += fresh.astype(jnp.float32)
        return fresh

    def user_phase(layer):
        phase = 2 * layer
        acc[layer % 2] = jnp.zeros(acc.shape[1:], acc.dtype)

        def step(pos, carry):
            base = stream(phase, pos)

            @pl.when(pos == 2)
            def _():
                unew[...] = user_rows(layer - 1)
                upan[col] = unew[...]
                for copy in user_sends(unew):
                    copy.start()

            @pl.when(pos == groups)
            def _():
                for g in range(groups):
                    give_panel(g).wait()

            where = item_rows(jnp.where(pos < groups, 0, 1), turn(phase, pos))
            user_product(layer, base, where)
            return carry

        lax.fori_loop(0, steps, step, 0)

    def give_copy(phase, q, k):
        slot = lax.rem(q, 2) * GROUP + k
        j = turn(phase, q) * GROUP + k
        return remote(ix_out.at[slot], ix_in.at[j], x_send.at[slot], x_recv.at[j], other)

    def item_phase(layer):
        phase = 2 * layer + 1
        final = layer == LAYERS - 1
        for copy in user_sends(user0 if layer == 0 else unew):
            copy.wait()
        for c in range(n_col):
            ut[:, c * own_rows:(c + 1) * own_rows] = upan[c].T
        for copy in shares(layer):
            copy.start()
        if final:
            own_panel(1).start()

        def give_step(pos, carry):
            base = stream(phase, pos)

            @pl.when(pos >= 2)
            def _():
                for k in range(GROUP):
                    give_copy(phase, pos - 2, k).wait_send()

            for k in range(GROUP):
                ix_out[lax.rem(pos, 2) * GROUP + k] = jnp.dot(ut[...], abuf[base + k], preferred_element_type=jnp.float32)
                give_copy(phase, pos, k).start()
            return carry

        lax.fori_loop(0, groups, give_step, 0)
        if final:
            own_panel(1).wait()

        def keep_step(pos, carry):
            base = stream(phase, pos)
            q = pos - groups
            g = turn(phase, pos)
            for k in range(GROUP):
                give_copy(phase, q, k).wait_recv()
            for k in range(GROUP):
                part = jnp.dot(ut[...], abuf[base + k], preferred_element_type=jnp.float32)
                fresh = (part + ix_in[g * GROUP + k]).astype(jnp.bfloat16).T
                at = pl.multiple_of(g * wide + k * KT, KT)
                here = pl.ds(at, KT)
                if layer == 0:
                    stash[here, :] = fresh
                if final:
                    total = panel[pl.ds(own_items + at, KT), :].astype(jnp.float32) + stash[here, :].astype(jnp.float32)
                    total = total + panel[here, :].astype(jnp.float32)
                    total = total + fresh.astype(jnp.float32)
                    fresh = (total / (LAYERS + 1)).astype(jnp.bfloat16)
                panel[here, :] = fresh
            if final:
                pltpu.make_async_copy(panel.at[item_rows(0, g), :], final_item.at[item_rows(0, g), :], f_sem.at[g]).start()
            else:
                give_panel(g).start()
            return carry

        lax.fori_loop(groups, steps, keep_step, 0)
        for q in range(groups - 2, groups):
            for k in range(GROUP):
                give_copy(phase, q, k).wait_send()

    item_phase(0)
    for layer in range(1, LAYERS):
        user_phase(layer)
        item_phase(layer)

    user_rows(LAYERS - 1)
    final = (user_sum[...] / (LAYERS + 1)).astype(jnp.bfloat16)
    final_user[...] = final
    share = picked.shape[0] // n_dev
    local = query[...] - (row * n_col + col) * own_rows
    hot = lax.broadcasted_iota(jnp.int32, (query.shape[0], own_rows), 1) == local
    mine[...] = jnp.dot(hot.astype(jnp.bfloat16), final, preferred_element_type=jnp.float32).astype(jnp.bfloat16)

    def rows_of(lin):
        return pl.ds(pl.multiple_of(lin * share, share), share)

    first = []
    for o in range(1, n_dev):
        lin, dest = device(o)
        first.append(remote(mine.at[rows_of(lin), :], parts.at[o - 1], one_send.at[o - 1], one_recv.at[o - 1], dest))
    for copy in first:
        copy.start()
    for copy in first:
        copy.wait()
    found = mine[rows_of(me), :].astype(jnp.float32)
    for o in range(1, n_dev):
        found = found + parts[o - 1].astype(jnp.float32)
    picked[rows_of(me), :] = found.astype(jnp.bfloat16)
    second = []
    for o in range(1, n_dev):
        here = picked.at[rows_of(me), :]
        second.append(remote(here, here, two_send.at[o - 1], two_recv.at[o - 1], device(o)[1]))
    for copy in second:
        copy.start()
    for copy in second:
        copy.wait()
    for g in range(groups):
        pltpu.make_async_copy(panel.at[item_rows(0, g), :], final_item.at[item_rows(0, g), :], f_sem.at[g]).wait()


def spread(bits, rs, cs, item_own, user_own, queries, n_col):
    items, emb = item_own.shape
    users = user_own.shape[0]
    rows, cols = n_col * users, cs.shape[1]
    chunks = cols // KT
    half = chunks // 2
    groups = half // GROUP
    n_dev = 2 * n_col
    n_query = queries.shape[0]
    anyspace = pl.BlockSpec(memory_space=pl.ANY)
    vmem = pl.BlockSpec(memory_space=pltpu.VMEM)
    dma = pltpu.SemaphoreType.DMA
    side = dma((n_col - 1,))
    all_dev = dma((n_dev - 1,))
    bf16, f32 = jnp.bfloat16, jnp.float32
    return pl.pallas_call(
        functools.partial(spread_kernel, n_col),
        in_specs=[anyspace, vmem, vmem, anyspace, vmem, vmem],
        out_specs=[anyspace, anyspace, vmem, vmem],
        out_shape=[jax.ShapeDtypeStruct((chunks, rows, KT), bf16),
                   jax.ShapeDtypeStruct((items, emb), bf16),
                   jax.ShapeDtypeStruct((users, emb), bf16),
                   jax.ShapeDtypeStruct((n_query, emb), bf16)],
        scratch_shapes=[
            pltpu.VMEM((3 * GROUP, rows, KT), bf16),
            pltpu.VMEM((2, rows // 16, GROUP * KT), jnp.int16),
            pltpu.VMEM((2 * items, emb), bf16),
            pltpu.VMEM((items, emb), bf16),
            pltpu.VMEM((2, rows, emb), f32),
            pltpu.VMEM((n_col, users, emb), bf16),
            pltpu.VMEM((emb, rows), bf16),
            pltpu.VMEM((users, emb), bf16),
            pltpu.VMEM((users, emb), f32),
            pltpu.VMEM((1, cols), f32),
            pltpu.VMEM((n_col - 1, users, emb), f32),
            pltpu.VMEM((half, emb, KT), f32),
            pltpu.VMEM((2 * GROUP, emb, KT), f32),
            pltpu.VMEM((n_query, emb), bf16),
            pltpu.VMEM((n_dev - 1, n_query // n_dev, emb), bf16),
            pltpu.VMEM((n_col - 1,) + rs.shape, jnp.int32),
            pltpu.VMEM(cs.shape, jnp.int32),
            dma((3,)), dma((2,)), dma((2,)), dma, dma, dma((groups,)), side, side, dma, dma,
            dma((groups,)), dma((groups,)), side, side, side, side, dma((2 * GROUP,)), dma((half,)),
            all_dev, all_dev, all_dev, all_dev,
        ],
        cost_estimate=pl.CostEstimate(flops=4 * LAYERS * rows * cols * emb, bytes_accessed=rows * cols * 10, transcendentals=0),
        compiler_params=pltpu.CompilerParams(collective_id=0, has_side_effects=True, vmem_limit_bytes=VMEM_CAP),
        name='spread',
    )(bits, rs, cs, item_own, user_own, queries[:, None])


def score_kernel(item, picked, final_item, scores):
    final_item[...] = item[...]
    scores[...] = lax.dot_general(picked[...], item[...], NT, preferred_element_type=jnp.float32)


def score(items, picked):
    rows, emb = items.shape
    n_query = picked.shape[0]
    tile = 1024 if rows % 1024 == 0 else rows
    block = pl.BlockSpec((tile, emb), lambda i: (i, 0))
    return pl.pallas_call(
        score_kernel,
        grid=(rows // tile,),
        in_specs=[block, pl.BlockSpec((n_query, emb), lambda i: (0, 0))],
        out_specs=[block, pl.BlockSpec((n_query, tile), lambda i: (0, i))],
        out_shape=[jax.ShapeDtypeStruct((rows, emb), jnp.bfloat16),
                   jax.ShapeDtypeStruct((n_query, rows), jnp.float32)],
        compiler_params=pltpu.CompilerParams(dimension_semantics=('arbitrary',), vmem_limit_bytes=VMEM_CAP),
        name='score',
    )(items, picked)


def solution(mesh):
    n_col = mesh.shape['col']

    def device_step(mask_blk, user_shard, item_shard, queries):
        bits, rs, cs = pack(mask_blk)
        _, item_sum, final_user, picked = spread(bits, rs, cs, item_shard, user_shard, queries, n_col)
        final_item, scores = score(item_sum, picked)
        return final_user, final_item, scores

    return jax.shard_map(device_step, mesh=mesh, in_specs=(P('row', 'col'), P(('row', 'col'), None), P(('col', 'row'), None), P()), out_specs=(P(('row', 'col'), None), P(('col', 'row'), None), P(None, ('col', 'row'))), check_vma=False)
```

time: 573 us -> 224 us (0.39); the launches traced: 567 us -> 224 us
  Pallas kernels: 0 us -> 220 us
  waiting for transfers between devices: 210 us -> 0 us
  matrix products: 197 us -> 0 us
  other arithmetic: 131 us -> 0 us
  between operations: 16.2 us -> 0.65 us
  blocking collectives: 9.35 us -> 0 us
    pallas_call x0 -> x3, Pallas kernels: none -> 220 us  [the longest x1 166 us: spread(): pl.pallas_call(functools.partial(spread_kernel, n_col), in_specs=[anyspac...]
    dot_general x7 -> x0, matrix products: 197 us -> none  [the longest x3 95.6 us: device_step(): lax.dot_general(norm_adj, user_panel, contract_rows, preferred_element_ty...]
    reduce_scatter x6 -> x0, waiting for transfers between devices: 106 us -> none  [the longest x3 61.4 us: device_step(): lax.psum_scatter(user_part, 'col', scatter_dimension=0, tiled=True)]
    convert_element_type x6 -> x0, other arithmetic: 88.6 us -> none  [the longest x1 64.1 us: norm_block(): (inv_user[:, None] * mask_blk.astype(jnp.float32) * inv_item[None, :]).as...]
    all_gather x6 -> x0, waiting for transfers between devices: 54.6 us -> none  [the longest x3 33.6 us: device_step(): item_panel = lax.all_gather(item_cur, 'row', axis=0, tiled=True)]
    psum x2 -> x0, waiting for transfers between devices: 47.8 us -> none  [the longest x1 42.7 us: query_scores(): picked = lax.psum(picked, ('row', 'col'))]
    reduce_sum x1 -> x0, other arithmetic: 40.8 us -> none  [norm_block(): deg_user = lax.psum(jnp.sum(mask_blk, axis=1), 'col')]
    psum x1 -> x0, blocking collectives: 9.35 us -> none  [norm_block(): deg_user = lax.psum(jnp.sum(mask_blk, axis=1), 'col')]
  transfers between devices with their start and end apart: 14 -> 0, of which waited for: 10 -> 0; matrix products, arithmetic and copies ran while one was open for 35% -> 0% of each run, Pallas kernels for 0% -> 0%
where the time goes in v2:
time: 224 us
  Pallas kernels  220 us (98%)
  local copies, waits for them, and re-layouts  3.2 us (1%)
    pallas_call x1, Pallas kernels, spread(): pl.pallas_call(functools.partial(spread_kernel, n_col), in_specs=[anyspac...  166 us
    pallas_call x1, Pallas kernels, pack(): pl.pallas_call(pack_kernel, in_specs=[anyspace], out_specs=[anyspace, vme...  43.3 us
    pallas_call x1, Pallas kernels, score(): pl.pallas_call(score_kernel, grid=(rows // tile,), in_specs=[block, pl.Bl...  10.6 us

profile of v2, /device:TPU:0, one launch (start us, length us, event | category | flops | bytes accessed | tf_op | source)
XLA Modules:
  0.0 224.1 jit_solution(10020382393521858160)
XLA Ops:
  0.6 1.5 copy.7.query
  2.2 43.3 %pack.1 = (s16[128,16384]{1,0:T(8,128)(2,1)}, s32[16,128]{1,0:T(8,128)}, s32[1,16384]{1,0:T(1,128)}) custom-call(s32[2048,16384]{1,0:T(8,128)} %mask.1), custom_call_target="tpu_custom_call" | custom-call | tf_op jit(solution)/shard_map/pack/pallas_call | solution.py:85
  45.5 166.3 %spread.1 = (bf16[32,2048,512]{2,1,0:T(8,128)(2,1)}, bf16[8192,256]{1,0:T(8,128)(2,1)}, bf16[512,256]{1,0:T(8,128)(2,1)}, bf16[512,256]{1,0:T(8,128)(2,1)}) custom-call(s16[128,16384]{1,0:T(8,128)(2,1)} %get-tuple-element.11.bits, s32[16,128]{1,0:T(8,128)} %get-tuple-element.12.rs_ref, s32[1,16384]{1,0:T(1,128)} %get-tuple-element.13.cs_ref, ...), custom_call_target="tpu_custom_call" | custom-call | flops 103079215104 | bytes 335544320 | tf_op jit(solution)/shard_map/spread/pallas_call | solution.py:457
  211.8 10.6 %score.1 = (bf16[8192,256]{1,0:T(8,128)(2,1)}, f32[512,8192]{1,0:T(8,128)}) custom-call(bf16[8192,256]{1,0:T(8,128)(2,1)} %get-tuple-element.15.item, bf16[512,256]{1,0:T(8,128)(2,1)} %get-tuple-element.16.picked), custom_call_target="tpu_custom_call" | custom-call | tf_op jit(solution)/shard_map/score/pallas_call | solution.py:503
  222.4 1.7 copy.9

commit v3 on v2

v3 whole, which is shorter than its diff:
```python
import functools

import jax
import jax.numpy as jnp
from jax import lax
from jax.experimental import pallas as pl
from jax.experimental.pallas import tpu as pltpu
from jax.sharding import PartitionSpec as P

LAYERS = 3
KT = 512
GROUP = 4
RING = 4
VMEM_CAP = 67043328
MESH = pl.DeviceIdType.MESH
NT = (((1,), (1,)), ((), ()))
TN = (((0,), (0,)), ((), ()))


def pack_kernel(mask, bits, rs_ref, cs_ref, buf, out, row_acc, in_sem, out_sem):
    rows, cols = mask.shape
    steps = cols // KT

    def columns(i):
        return pl.ds(pl.multiple_of(i * KT, KT), KT)

    def load(i):
        slot = lax.rem(i, RING)
        return pltpu.make_async_copy(mask.at[:, columns(i)], buf.at[slot], in_sem.at[slot])

    def save(i):
        slot = lax.rem(i, 2)
        return pltpu.make_async_copy(out.at[slot], bits.at[i], out_sem.at[slot])

    for i in range(RING - 1):
        load(i).start()
    row_acc[...] = jnp.zeros_like(row_acc)

    def step(i, carry):
        slot = lax.rem(i, RING)

        @pl.when(i + RING - 1 < steps)
        def _():
            load(i + RING - 1).start()

        @pl.when(i >= 2)
        def _():
            save(i - 2).wait()

        load(i).wait()

        def block(b, col_acc):
            words = []
            for k in range(2):
                word = jnp.zeros((8, KT), jnp.int32)
                for j in range(16):
                    at = pl.ds(pl.multiple_of(b * 256 + j * 16 + k * 8, 8), 8)
                    m = buf[slot, at, :]
                    word = word | (lax.shift_left(m, j) if j else m)
                    col_acc = col_acc + m
                    part = m[:, :128]
                    for t in range(1, KT // 128):
                        part = part + m[:, t * 128:(t + 1) * 128]
                    row_acc[at, :] += part
                words.append(word)
            out[lax.rem(i, 2), pl.ds(pl.multiple_of(b * 16, 16), 16), :] = jnp.concatenate(words, axis=0).astype(jnp.int16)
            return col_acc

        col_acc = lax.fori_loop(0, rows // 256, block, jnp.zeros((8, KT), jnp.int32))
        cs_ref[:, columns(i)] = jnp.sum(col_acc, axis=0, keepdims=True)
        save(i).start()
        return carry

    lax.fori_loop(0, steps, step, 0)
    for g in range(rows // 128):
        rs_ref[g:g + 1, :] = jnp.sum(row_acc[g * 128:(g + 1) * 128, :].T, axis=0, keepdims=True)
    save(steps - 2).wait()
    save(steps - 1).wait()


def pack(mask_blk):
    rows, cols = mask_blk.shape
    steps = cols // KT
    vmem = pl.BlockSpec(memory_space=pltpu.VMEM)
    anyspace = pl.BlockSpec(memory_space=pl.ANY)
    return pl.pallas_call(
        pack_kernel,
        in_specs=[anyspace],
        out_specs=[anyspace, vmem, vmem],
        out_shape=[jax.ShapeDtypeStruct((steps, rows // 16, KT), jnp.int16),
                   jax.ShapeDtypeStruct((rows // 128, 128), jnp.int32),
                   jax.ShapeDtypeStruct((1, cols), jnp.int32)],
        scratch_shapes=[pltpu.VMEM((RING, rows, KT), jnp.int32), pltpu.VMEM((2, rows // 16, KT), jnp.int16),
                        pltpu.VMEM((rows, 128), jnp.int32),
                        pltpu.SemaphoreType.DMA((RING,)), pltpu.SemaphoreType.DMA((2,))],
        compiler_params=pltpu.CompilerParams(vmem_limit_bytes=VMEM_CAP),
        name='pack',
    )(mask_blk)


def greet(peers):
    barrier = pltpu.get_barrier_semaphore()
    for dev in peers:
        pl.semaphore_signal(barrier, inc=1, device_id=dev, device_id_type=MESH)
    pl.semaphore_wait(barrier, len(peers))


def expand(bits, du, di, place, b):
    lanes = di.shape[1] // 128
    wide = jnp.concatenate([du[b * 256:(b + 1) * 256, :]] * lanes, axis=1)
    word = jnp.concatenate([bits[b * 16:(b + 1) * 16, :]] * 16, axis=0)
    hit = (word & jnp.concatenate([place[...]] * lanes, axis=1)) != 0
    value = (wide * di).astype(jnp.bfloat16)
    return jnp.where(hit, value, jnp.zeros_like(value))


def spread_kernel(n_col, bits, rs_ref, cs_ref, item0, user0, query, final_item, final_user, picked,
                  words, du, place, panel, stash, acc, upan, ut, unew, user_sum, di, rs_in, ix_in, ix_out, mine, parts,
                  deg_in, cnt_in,
                  b_sem, own_sem, f_sem, deg_send, deg_recv, cnt_send, cnt_recv,
                  p_send, p_recv, u_send, u_recv, r_send, r_recv, x_send, x_recv, one_send, one_recv, two_send, two_recv):
    col, row = lax.axis_index('col'), lax.axis_index('row')
    other = (col, 1 - row)
    n_dev = 2 * n_col
    chunks = bits.shape[0]
    half = chunks // 2
    groups = half // GROUP
    steps = 2 * groups
    rows, emb = acc.shape[1], acc.shape[2]
    wide = GROUP * KT
    own_items = half * KT
    own_rows = rows // n_col
    sides = [(lax.rem(col + o, n_col), row) for o in range(1, n_col)]
    me = col * 2 + row

    def device(o):
        lin = lax.rem(me + o, n_dev)
        return lin, (lin // 2, lin % 2)

    def remote(src, dst, send, recv, dest):
        return pltpu.make_async_remote_copy(src_ref=src, dst_ref=dst, send_sem=send, recv_sem=recv,
                                            device_id=dest, device_id_type=MESH)

    greet([device(o)[1] for o in range(1, n_dev)])

    counts = [remote(cs_ref, cnt_in, cnt_send, cnt_recv, other)]
    counts += [remote(rs_ref, deg_in.at[i], deg_send.at[i], deg_recv.at[i], sides[i]) for i in range(n_col - 1)]
    for copy in counts:
        copy.start()

    def turn(phase, pos):
        return lax.rem(phase + pos, groups)

    def item_rows(side, g):
        return pl.ds(pl.multiple_of(side * own_items + g * wide, wide), wide)

    def give_panel(g):
        return remote(panel.at[item_rows(0, g), :], panel.at[item_rows(1, g), :], p_send.at[g], p_recv.at[g], other)

    def first_panel(g):
        return remote(item0.at[item_rows(0, g), :], panel.at[item_rows(1, g), :], p_send.at[g], p_recv.at[g], other)

    def own_panel(side):
        return pltpu.make_async_copy(item0, panel.at[pl.ds(side * own_items, own_items), :], own_sem)

    def chunk_of(near, g):
        return jnp.where(near, row, 1 - row) * half + g * GROUP

    words_copy = pltpu.make_async_copy(bits, words, b_sem)
    words_copy.start()
    own_panel(0).start()
    for g in range(groups):
        first_panel(g).start()

    def user_sends(src):
        return [remote(src, upan.at[col], u_send.at[i], u_recv.at[i], sides[i]) for i in range(n_col - 1)]

    for copy in user_sends(user0):
        copy.start()
    upan[col] = user0[...]
    for j in range(16):
        place[j * 16:(j + 1) * 16, :] = jnp.full((16, 128), 1 << j if j < 15 else -32768, jnp.int16)
    user_sum[...] = user0[...].astype(jnp.float32)

    for copy in counts:
        copy.wait()
    degree = rs_ref[...]
    for i in range(n_col - 1):
        degree = degree + deg_in[i]
    inv_user = lax.rsqrt(jnp.maximum(degree, 1).astype(jnp.float32))
    for g in range(rows // 128):
        du[g * 128:(g + 1) * 128, :] = jnp.broadcast_to(inv_user[g:g + 1, :], (128, 128)).T
    di[...] = lax.rsqrt(jnp.maximum(cs_ref[...] + cnt_in[...], 1).astype(jnp.float32))

    def scale_of(chunk):
        return di[:, pl.ds(pl.multiple_of(chunk * KT, KT), KT)]

    def user_product(layer, chunk, where):
        scale = [scale_of(chunk + k) for k in range(GROUP)]
        for b in range(rows // 256):
            left = jnp.concatenate([expand(words.at[chunk + k], du, scale[k], place, b) for k in range(GROUP)], axis=1)
            acc[layer % 2, b * 256:(b + 1) * 256, :] += jnp.dot(left, panel[where, :], preferred_element_type=jnp.float32)

    def item_product(chunk):
        scale = scale_of(chunk)
        right = jnp.concatenate([expand(words.at[chunk], du, scale, place, b) for b in range(rows // 256)], axis=0)
        return jnp.dot(ut[...], right, preferred_element_type=jnp.float32)

    def phase_chunk(phase, pos):
        users_first = phase % 2 == 0
        near = (pos < groups) == users_first
        return chunk_of(near, turn(phase, pos))

    def shares(layer):
        out = []
        for i in range(n_col - 1):
            at = pl.multiple_of(sides[i][0] * own_rows, own_rows)
            out.append(remote(acc.at[layer % 2, pl.ds(at, own_rows), :], rs_in.at[i], r_send.at[i], r_recv.at[i], sides[i]))
        return out

    def user_rows(layer):
        for copy in shares(layer):
            copy.wait()
        total = acc[layer % 2, pl.ds(pl.multiple_of(col * own_rows, own_rows), own_rows), :]
        for i in range(n_col - 1):
            total = total + rs_in[i]
        fresh = total.astype(jnp.bfloat16)
        user_sum[...] += fresh.astype(jnp.float32)
        return fresh

    def user_phase(layer):
        phase = 2 * layer
        acc[layer % 2] = jnp.zeros(acc.shape[1:], acc.dtype)

        def step(pos, carry):
            def next_users():
                unew[...] = user_rows(layer - 1)
                upan[col] = unew[...]
                for copy in user_sends(unew):
                    copy.start()

            if layer > 0:
                pl.when(pos == 2)(next_users)

            @pl.when(pos == groups)
            def _():
                for g in range(groups):
                    (give_panel if layer > 0 else first_panel)(g).wait()

            where = item_rows(jnp.where(pos < groups, 0, 1), turn(phase, pos))
            user_product(layer, phase_chunk(phase, pos), where)
            return carry

        lax.fori_loop(0, steps, step, 0)

    def part_slot(pos):
        return lax.rem(pos, 3) * GROUP

    def give_copy(phase, q, k):
        slot = part_slot(q) + k
        j = turn(phase, q) * GROUP + k
        return remote(ix_out.at[slot], ix_in.at[j], x_send.at[slot], x_recv.at[j], other)

    def item_phase(layer):
        phase = 2 * layer + 1
        final = layer == LAYERS - 1
        for copy in user_sends(user0 if layer == 0 else unew):
            copy.wait()
        for c in range(n_col):
            ut[:, c * own_rows:(c + 1) * own_rows] = upan[c].T
        for copy in shares(layer):
            copy.start()
        if final:
            own_panel(1).start()

        def product(pos, base, k):
            ix_out[part_slot(pos) + k] = item_product(base + k)

        def sent(pos):
            for k in range(GROUP):
                give_copy(phase, pos - 3, k).wait_send()

        def give_step(pos, carry):
            base = phase_chunk(phase, pos)
            pl.when(pos >= 3)(functools.partial(sent, pos))
            for k in range(GROUP):
                product(pos, base, k)
                give_copy(phase, pos, k).start()
            return carry

        def arrived(pos):
            for k in range(GROUP):
                give_copy(phase, pos - groups, k).wait_recv()

        def finish(pos, k):
            g = turn(phase, pos)
            fresh = (ix_out[part_slot(pos) + k] + ix_in[g * GROUP + k]).astype(jnp.bfloat16).T
            at = pl.multiple_of(g * wide + k * KT, KT)
            here = pl.ds(at, KT)
            if layer == 0:
                stash[here, :] = fresh
            if final:
                total = panel[pl.ds(own_items + at, KT), :].astype(jnp.float32) + stash[here, :].astype(jnp.float32)
                total = total + panel[here, :].astype(jnp.float32)
                total = total + fresh.astype(jnp.float32)
                fresh = (total / (LAYERS + 1)).astype(jnp.bfloat16)
            panel[here, :] = fresh

        def hand_on(pos):
            g = turn(phase, pos)
            if final:
                pltpu.make_async_copy(panel.at[item_rows(0, g), :], final_item.at[item_rows(0, g), :], f_sem.at[g]).start()
            else:
                give_panel(g).start()

        def keep_step(pos, carry):
            base = phase_chunk(phase, pos)

            @pl.when(pos < groups + 3)
            def _():
                sent(pos)

            arrived(pos - 1)
            for k in range(GROUP):
                finish(pos - 1, k)
                product(pos, base, k)
            hand_on(pos - 1)
            return carry

        lax.fori_loop(0, groups, give_step, 0)
        if final:
            own_panel(1).wait()
        base = phase_chunk(phase, groups)
        sent(groups)
        for k in range(GROUP):
            product(groups, base, k)
        lax.fori_loop(groups + 1, steps, keep_step, 0)
        arrived(steps - 1)
        for k in range(GROUP):
            finish(steps - 1, k)
        hand_on(steps - 1)

    words_copy.wait()
    own_panel(0).wait()
    for layer in range(LAYERS):
        user_phase(layer)
        item_phase(layer)

    user_rows(LAYERS - 1)
    final = (user_sum[...] / (LAYERS + 1)).astype(jnp.bfloat16)
    final_user[...] = final
    share = picked.shape[0] // n_dev
    local = query[...] - (row * n_col + col) * own_rows
    hot = lax.broadcasted_iota(jnp.int32, (own_rows, query.shape[1]), 0) == local
    mine[...] = lax.dot_general(hot.astype(jnp.bfloat16), final, TN, preferred_element_type=jnp.float32).astype(jnp.bfloat16)

    def rows_of(lin):
        return pl.ds(pl.multiple_of(lin * share, share), share)

    first = []
    for o in range(1, n_dev):
        lin, dest = device(o)
        first.append(remote(mine.at[rows_of(lin), :], parts.at[o - 1], one_send.at[o - 1], one_recv.at[o - 1], dest))
    for copy in first:
        copy.start()
    for copy in first:
        copy.wait()
    found = mine[rows_of(me), :].astype(jnp.float32)
    for o in range(1, n_dev):
        found = found + parts[o - 1].astype(jnp.float32)
    picked[rows_of(me), :] = found.astype(jnp.bfloat16)
    second = []
    for o in range(1, n_dev):
        here = picked.at[rows_of(me), :]
        second.append(remote(here, here, two_send.at[o - 1], two_recv.at[o - 1], device(o)[1]))
    for copy in second:
        copy.start()
    for copy in second:
        copy.wait()
    for g in range(groups):
        pltpu.make_async_copy(panel.at[item_rows(0, g), :], final_item.at[item_rows(0, g), :], f_sem.at[g]).wait()


def spread(bits, rs, cs, item_own, user_own, queries, n_col):
    items, emb = item_own.shape
    users = user_own.shape[0]
    rows, cols = n_col * users, cs.shape[1]
    chunks = cols // KT
    half = chunks // 2
    groups = half // GROUP
    n_dev = 2 * n_col
    n_query = queries.shape[0]
    anyspace = pl.BlockSpec(memory_space=pl.ANY)
    vmem = pl.BlockSpec(memory_space=pltpu.VMEM)
    dma = pltpu.SemaphoreType.DMA
    side = dma((n_col - 1,))
    all_dev = dma((n_dev - 1,))
    bf16, f32 = jnp.bfloat16, jnp.float32
    return pl.pallas_call(
        functools.partial(spread_kernel, n_col),
        in_specs=[anyspace, vmem, vmem, anyspace, vmem, vmem],
        out_specs=[anyspace, vmem, vmem],
        out_shape=[jax.ShapeDtypeStruct((items, emb), bf16),
                   jax.ShapeDtypeStruct((users, emb), bf16),
                   jax.ShapeDtypeStruct((n_query, emb), bf16)],
        scratch_shapes=[
            pltpu.VMEM(bits.shape, jnp.int16),
            pltpu.VMEM((rows, 128), f32),
            pltpu.VMEM((256, 128), jnp.int16),
            pltpu.VMEM((2 * items, emb), bf16),
            pltpu.VMEM((items, emb), bf16),
            pltpu.VMEM((2, rows, emb), f32),
            pltpu.VMEM((n_col, users, emb), bf16),
            pltpu.VMEM((emb, rows), bf16),
            pltpu.VMEM((users, emb), bf16),
            pltpu.VMEM((users, emb), f32),
            pltpu.VMEM((1, cols), f32),
            pltpu.VMEM((n_col - 1, users, emb), f32),
            pltpu.VMEM((half, emb, KT), f32),
            pltpu.VMEM((3 * GROUP, emb, KT), f32),
            pltpu.VMEM((n_query, emb), bf16),
            pltpu.VMEM((n_dev - 1, n_query // n_dev, emb), bf16),
            pltpu.VMEM((n_col - 1,) + rs.shape, jnp.int32),
            pltpu.VMEM(cs.shape, jnp.int32),
            dma, dma, dma((groups,)), side, side, dma, dma,
            dma((groups,)), dma((groups,)), side, side, side, side, dma((3 * GROUP,)), dma((half,)),
            all_dev, all_dev, all_dev, all_dev,
        ],
        cost_estimate=pl.CostEstimate(flops=4 * LAYERS * rows * cols * emb, bytes_accessed=rows * cols, transcendentals=0),
        compiler_params=pltpu.CompilerParams(collective_id=0, has_side_effects=True, vmem_limit_bytes=VMEM_CAP),
        name='spread',
    )(bits, rs, cs, item_own, user_own, queries[None, :])


def score_kernel(user, item, picked, final_user, final_item, scores):
    final_user[...] = user[...]
    final_item[...] = item[...]
    scores[...] = lax.dot_general(picked[...], item[...], NT, preferred_element_type=jnp.float32)


def score(users, items, picked):
    rows, emb = items.shape
    n_query = picked.shape[0]
    tile = 1024 if rows % 1024 == 0 else rows
    block = pl.BlockSpec((tile, emb), lambda i: (i, 0))
    whole = pl.BlockSpec(users.shape, lambda i: (0, 0))
    return pl.pallas_call(
        score_kernel,
        grid=(rows // tile,),
        in_specs=[whole, block, pl.BlockSpec((n_query, emb), lambda i: (0, 0))],
        out_specs=[whole, block, pl.BlockSpec((n_query, tile), lambda i: (0, i))],
        out_shape=[jax.ShapeDtypeStruct(users.shape, jnp.bfloat16),
                   jax.ShapeDtypeStruct((rows, emb), jnp.bfloat16),
                   jax.ShapeDtypeStruct((n_query, rows), jnp.float32)],
        compiler_params=pltpu.CompilerParams(dimension_semantics=('arbitrary',), vmem_limit_bytes=VMEM_CAP),
        name='score',
    )(users, items, picked)


def solution(mesh):
    n_col = mesh.shape['col']

    def device_step(mask_blk, user_shard, item_shard, queries):
        bits, rs, cs = pack(mask_blk)
        item_mean, user_mean, picked = spread(bits, rs, cs, item_shard, user_shard, queries, n_col)
        final_user, final_item, scores = score(user_mean, item_mean, picked)
        return final_user, final_item, scores

    return jax.shard_map(device_step, mesh=mesh, in_specs=(P('row', 'col'), P(('row', 'col'), None), P(('col', 'row'), None), P()), out_specs=(P(('row', 'col'), None), P(('col', 'row'), None), P(None, ('col', 'row'))), check_vma=False)
```

time: 224 us -> 207 us (0.924)
  Pallas kernels: 220 us -> 206 us
  local copies, waits for them, and re-layouts: 3.2 us -> 0 us
    pallas_call x1, Pallas kernels: 166 us -> 151 us  [spread(): pl.pallas_call(functools.partial(spread_kernel, n_col), in_specs=[anyspac...]
where the time goes in v3:
time: 207 us; the launch traced here: 206 us
  Pallas kernels  206 us (100%)
    pallas_call x1, Pallas kernels, spread(): pl.pallas_call(functools.partial(spread_kernel, n_col), in_specs=[anyspac...  151 us
    pallas_call x1, Pallas kernels, pack(): pl.pallas_call(pack_kernel, in_specs=[anyspace], out_specs=[anyspace, vme...  43.3 us
    pallas_call x1, Pallas kernels, score(): pl.pallas_call(score_kernel, grid=(rows // tile,), in_specs=[whole, block...  10.8 us

profile of v3, /device:TPU:0, one launch (start us, length us, event | category | flops | bytes accessed | tf_op | source)
XLA Modules:
  0.0 206.2 jit_solution(9144039181264714192)
XLA Ops:
  0.6 43.3 %pack.1 = (s16[32,128,512]{2,1,0:T(8,128)(2,1)}, s32[16,128]{1,0:T(8,128)}, s32[1,16384]{1,0:T(1,128)}) custom-call(s32[2048,16384]{1,0:T(8,128)} %mask.1), custom_call_target="tpu_custom_call" | custom-call | tf_op jit(solution)/shard_map/pack/pallas_call | solution.py:86
  44.0 151.5 %spread.1 = (bf16[8192,256]{1,0:T(8,128)(2,1)}, bf16[512,256]{1,0:T(8,128)(2,1)}, bf16[512,256]{1,0:T(8,128)(2,1)}) custom-call(s16[32,128,512]{2,1,0:T(8,128)(2,1)} %get-tuple-element.9.bits, s32[16,128]{1,0:T(8,128)} %get-tuple-element.10.rs_ref, s32[1,16384]{1,0:T(1,128)} %get-tuple-element.11.cs_ref, bf16[8192,256]{1,0:T(8,128)(2,1)} %item0.1, ...), custom_call_target="tpu_custom_call" | custom-call | flops 103079215104 | bytes 33554432 | tf_op jit(solution)/shard_map/spread/pallas_call | solution.py:399
  195.4 10.8 %score.1 = (bf16[512,256]{1,0:T(8,128)(2,1)}, bf16[8192,256]{1,0:T(8,128)(2,1)}, f32[512,8192]{1,0:T(8,128)}) custom-call(bf16[512,256]{1,0:T(8,128)(2,1)} %get-tuple-element.12.user, bf16[8192,256]{1,0:T(8,128)(2,1)} %get-tuple-element.13.item, bf16[512,256]{1,0:T(8,128)(2,1)} %get-tuple-element.14.picked), custom_call_target="tpu_custom_call" | custom-call | tf_op jit(solution)/shard_map/score/pallas_call | solution.py:447

commit v4 on v3

--- a/solution.py
+++ b/solution.py
@@ -10,31 +10,18 @@
 LAYERS = 3
 KT = 512
 GROUP = 4
-RING = 4
+RING = 3
 VMEM_CAP = 67043328
 MESH = pl.DeviceIdType.MESH
 NT = (((1,), (1,)), ((), ()))
 TN = (((0,), (0,)), ((), ()))
 
 
-def pack_kernel(mask, bits, rs_ref, cs_ref, buf, out, row_acc, in_sem, out_sem):
+def pack(mask, words, rs_ref, cs_ref, buf, row_acc, load):
     rows, cols = mask.shape
     steps = cols // KT
-
-    def columns(i):
-        return pl.ds(pl.multiple_of(i * KT, KT), KT)
-
-    def load(i):
-        slot = lax.rem(i, RING)
-        return pltpu.make_async_copy(mask.at[:, columns(i)], buf.at[slot], in_sem.at[slot])
-
-    def save(i):
-        slot = lax.rem(i, 2)
-        return pltpu.make_async_copy(out.at[slot], bits.at[i], out_sem.at[slot])
-
-    for i in range(RING - 1):
-        load(i).start()
     row_acc[...] = jnp.zeros_like(row_acc)
+    shift_of = lax.broadcasted_iota(jnp.int32, (256, KT), 0) // 16
 
     def step(i, carry):
         slot = lax.rem(i, RING)
@@ -43,59 +30,26 @@
         def _():
             load(i + RING - 1).start()
 
-        @pl.when(i >= 2)
-        def _():
-            save(i - 2).wait()
-
         load(i).wait()
 
         def block(b, col_acc):
-            words = []
-            for k in range(2):
-                word = jnp.zeros((8, KT), jnp.int32)
-                for j in range(16):
-                    at = pl.ds(pl.multiple_of(b * 256 + j * 16 + k * 8, 8), 8)
-                    m = buf[slot, at, :]
-                    word = word | (lax.shift_left(m, j) if j else m)
-                    col_acc = col_acc + m
-                    part = m[:, :128]
-                    for t in range(1, KT // 128):
-                        part = part + m[:, t * 128:(t + 1) * 128]
-                    row_acc[at, :] += part
-                words.append(word)
-            out[lax.rem(i, 2), pl.ds(pl.multiple_of(b * 16, 16), 16), :] = jnp.concatenate(words, axis=0).astype(jnp.int16)
-            return col_acc
+            at = pl.ds(pl.multiple_of(b * 256, 256), 256)
+            m = buf[slot, at, :]
+            part = m[:, :128]
+            for t in range(1, KT // 128):
+                part = part + m[:, t * 128:(t + 1) * 128]
+            row_acc[at, :] += part
+            weighed = (m << shift_of).reshape(16, 16, KT)
+            words[i, pl.ds(pl.multiple_of(b * 16, 16), 16), :] = jnp.sum(weighed, axis=0).astype(jnp.int16)
+            return col_acc + jnp.sum(m.reshape(32, 8, KT), axis=0)
 
         col_acc = lax.fori_loop(0, rows // 256, block, jnp.zeros((8, KT), jnp.int32))
-        cs_ref[:, columns(i)] = jnp.sum(col_acc, axis=0, keepdims=True)
-        save(i).start()
+        cs_ref[:, pl.ds(pl.multiple_of(i * KT, KT), KT)] = jnp.sum(col_acc, axis=0, keepdims=True)
         return carry
 
     lax.fori_loop(0, steps, step, 0)
     for g in range(rows // 128):
         rs_ref[g:g + 1, :] = jnp.sum(row_acc[g * 128:(g + 1) * 128, :].T, axis=0, keepdims=True)
-    save(steps - 2).wait()
-    save(steps - 1).wait()
-
-
-def pack(mask_blk):
-    rows, cols = mask_blk.shape
-    steps = cols // KT
-    vmem = pl.BlockSpec(memory_space=pltpu.VMEM)
-    anyspace = pl.BlockSpec(memory_space=pl.ANY)
-    return pl.pallas_call(
-        pack_kernel,
-        in_specs=[anyspace],
-        out_specs=[anyspace, vmem, vmem],
-        out_shape=[jax.ShapeDtypeStruct((steps, rows // 16, KT), jnp.int16),
-                   jax.ShapeDtypeStruct((rows // 128, 128), jnp.int32),
-                   jax.ShapeDtypeStruct((1, cols), jnp.int32)],
-        scratch_shapes=[pltpu.VMEM((RING, rows, KT), jnp.int32), pltpu.VMEM((2, rows // 16, KT), jnp.int16),
-                        pltpu.VMEM((rows, 128), jnp.int32),
-                        pltpu.SemaphoreType.DMA((RING,)), pltpu.SemaphoreType.DMA((2,))],
-        compiler_params=pltpu.CompilerParams(vmem_limit_bytes=VMEM_CAP),
-        name='pack',
-    )(mask_blk)
 
 
 def greet(peers):
@@ -114,15 +68,15 @@
     return jnp.where(hit, value, jnp.zeros_like(value))
 
 
-def spread_kernel(n_col, bits, rs_ref, cs_ref, item0, user0, query, final_item, final_user, picked,
-                  words, du, place, panel, stash, acc, upan, ut, unew, user_sum, di, rs_in, ix_in, ix_out, mine, parts,
+def spread_kernel(n_col, mask, item0, user0, query, final_item, final_user, picked,
+                  buf, row_acc, rs_ref, cs_ref, words, du, place, panel, stash, acc, upan, ut, unew, user_sum, di, rs_in, ix_in, ix_out, mine, parts,
                   deg_in, cnt_in,
-                  b_sem, own_sem, f_sem, deg_send, deg_recv, cnt_send, cnt_recv,
+                  m_sem, own_sem, f_sem, deg_send, deg_recv, cnt_send, cnt_recv,
                   p_send, p_recv, u_send, u_recv, r_send, r_recv, x_send, x_recv, one_send, one_recv, two_send, two_recv):
     col, row = lax.axis_index('col'), lax.axis_index('row')
     other = (col, 1 - row)
     n_dev = 2 * n_col
-    chunks = bits.shape[0]
+    chunks = mask.shape[1] // KT
     half = chunks // 2
     groups = half // GROUP
     steps = 2 * groups
@@ -141,36 +95,13 @@
         return pltpu.make_async_remote_copy(src_ref=src, dst_ref=dst, send_sem=send, recv_sem=recv,
                                             device_id=dest, device_id_type=MESH)
 
+    def load(i):
+        slot = lax.rem(i, RING)
+        return pltpu.make_async_copy(mask.at[:, pl.ds(pl.multiple_of(i * KT, KT), KT)], buf.at[slot], m_sem.at[slot])
+
+    for i in range(RING - 1):
+        load(jnp.int32(i)).start()
     greet([device(o)[1] for o in range(1, n_dev)])
-
-    counts = [remote(cs_ref, cnt_in, cnt_send, cnt_recv, other)]
-    counts += [remote(rs_ref, deg_in.at[i], deg_send.at[i], deg_recv.at[i], sides[i]) for i in range(n_col - 1)]
-    for copy in counts:
-        copy.start()
-
-    def turn(phase, pos):
-        return lax.rem(phase + pos, groups)
-
-    def item_rows(side, g):
-        return pl.ds(pl.multiple_of(side * own_items + g * wide, wide), wide)
-
-    def give_panel(g):
-        return remote(panel.at[item_rows(0, g), :], panel.at[item_rows(1, g), :], p_send.at[g], p_recv.at[g], other)
-
-    def first_panel(g):
-        return remote(item0.at[item_rows(0, g), :], panel.at[item_rows(1, g), :], p_send.at[g], p_recv.at[g], other)
-
-    def own_panel(side):
-        return pltpu.make_async_copy(item0, panel.at[pl.ds(side * own_items, own_items), :], own_sem)
-
-    def chunk_of(near, g):
-        return jnp.where(near, row, 1 - row) * half + g * GROUP
-
-    words_copy = pltpu.make_async_copy(bits, words, b_sem)
-    words_copy.start()
-    own_panel(0).start()
-    for g in range(groups):
-        first_panel(g).start()
 
     def user_sends(src):
         return [remote(src, upan.at[col], u_send.at[i], u_recv.at[i], sides[i]) for i in range(n_col - 1)]
@@ -181,6 +112,34 @@
     for j in range(16):
         place[j * 16:(j + 1) * 16, :] = jnp.full((16, 128), 1 << j if j < 15 else -32768, jnp.int16)
     user_sum[...] = user0[...].astype(jnp.float32)
+    pack(mask, words, rs_ref, cs_ref, buf, row_acc, load)
+
+    counts = [remote(cs_ref, cnt_in, cnt_send, cnt_recv, other)]
+    counts += [remote(rs_ref, deg_in.at[i], deg_send.at[i], deg_recv.at[i], sides[i]) for i in range(n_col - 1)]
+    for copy in counts:
+        copy.start()
+
+    def turn(phase, pos):
+        return lax.rem(phase + pos, groups)
+
+    def item_rows(side, g):
+        return pl.ds(pl.multiple_of(side * own_items + g * wide, wide), wide)
+
+    def give_panel(g):
+        return remote(panel.at[item_rows(0, g), :], panel.at[item_rows(1, g), :], p_send.at[g], p_recv.at[g], other)
+
+    def first_panel(g):
+        return remote(item0.at[item_rows(0, g), :], panel.at[item_rows(1, g), :], p_send.at[g], p_recv.at[g], other)
+
+    def own_panel(side):
+        return pltpu.make_async_copy(item0, panel.at[pl.ds(side * own_items, own_items), :], own_sem)
+
+    def chunk_of(near, g):
+        return jnp.where(near, row, 1 - row) * half + g * GROUP
+
+    own_panel(0).start()
+    for g in range(groups):
+        first_panel(g).start()
 
     for copy in counts:
         copy.wait()
@@ -340,7 +299,6 @@
             finish(steps - 1, k)
         hand_on(steps - 1)
 
-    words_copy.wait()
     own_panel(0).wait()
     for layer in range(LAYERS):
         user_phase(layer)
@@ -381,10 +339,10 @@
         pltpu.make_async_copy(panel.at[item_rows(0, g), :], final_item.at[item_rows(0, g), :], f_sem.at[g]).wait()
 
 
-def spread(bits, rs, cs, item_own, user_own, queries, n_col):
+def spread(mask_blk, item_own, user_own, queries, n_col):
     items, emb = item_own.shape
     users = user_own.shape[0]
-    rows, cols = n_col * users, cs.shape[1]
+    rows, cols = mask_blk.shape
     chunks = cols // KT
     half = chunks // 2
     groups = half // GROUP
@@ -398,13 +356,17 @@
     bf16, f32 = jnp.bfloat16, jnp.float32
     return pl.pallas_call(
         functools.partial(spread_kernel, n_col),
-        in_specs=[anyspace, vmem, vmem, anyspace, vmem, vmem],
+        in_specs=[anyspace, anyspace, vmem, vmem],
         out_specs=[anyspace, vmem, vmem],
         out_shape=[jax.ShapeDtypeStruct((items, emb), bf16),
                    jax.ShapeDtypeStruct((users, emb), bf16),
                    jax.ShapeDtypeStruct((n_query, emb), bf16)],
         scratch_shapes=[
-            pltpu.VMEM(bits.shape, jnp.int16),
+            pltpu.VMEM((RING, rows, KT), jnp.int32),
+            pltpu.VMEM((rows, 128), jnp.int32),
+            pltpu.VMEM((rows // 128, 128), jnp.int32),
+            pltpu.VMEM((1, cols), jnp.int32),
+            pltpu.VMEM((chunks, rows // 16, KT), jnp.int16),
             pltpu.VMEM((rows, 128), f32),
             pltpu.VMEM((256, 128), jnp.int16),
             pltpu.VMEM((2 * items, emb), bf16),
@@ -420,16 +382,16 @@
             pltpu.VMEM((3 * GROUP, emb, KT), f32),
             pltpu.VMEM((n_query, emb), bf16),
             pltpu.VMEM((n_dev - 1, n_query // n_dev, emb), bf16),
-            pltpu.VMEM((n_col - 1,) + rs.shape, jnp.int32),
-            pltpu.VMEM(cs.shape, jnp.int32),
-            dma, dma, dma((groups,)), side, side, dma, dma,
+            pltpu.VMEM((n_col - 1, rows // 128, 128), jnp.int32),
+            pltpu.VMEM((1, cols), jnp.int32),
+            dma((RING,)), dma, dma((groups,)), side, side, dma, dma,
             dma((groups,)), dma((groups,)), side, side, side, side, dma((3 * GROUP,)), dma((half,)),
             all_dev, all_dev, all_dev, all_dev,
         ],
-        cost_estimate=pl.CostEstimate(flops=4 * LAYERS * rows * cols * emb, bytes_accessed=rows * cols, transcendentals=0),
+        cost_estimate=pl.CostEstimate(flops=4 * LAYERS * rows * cols * emb, bytes_accessed=rows * cols * 4, transcendentals=0),
         compiler_params=pltpu.CompilerParams(collective_id=0, has_side_effects=True, vmem_limit_bytes=VMEM_CAP),
         name='spread',
-    )(bits, rs, cs, item_own, user_own, queries[None, :])
+    )(mask_blk, item_own, user_own, queries[None, :])
 
 
 def score_kernel(user, item, picked, final_user, final_item, scores):
@@ -441,7 +403,7 @@
 def score(users, items, picked):
     rows, emb = items.shape
     n_query = picked.shape[0]
-    tile = 1024 if rows % 1024 == 0 else rows
+    tile = 2048 if rows % 2048 == 0 else rows
     block = pl.BlockSpec((tile, emb), lambda i: (i, 0))
     whole = pl.BlockSpec(users.shape, lambda i: (0, 0))
     return pl.pallas_call(
@@ -461,8 +423,7 @@
     n_col = mesh.shape['col']
 
     def device_step(mask_blk, user_shard, item_shard, queries):
-        bits, rs, cs = pack(mask_blk)
-        item_mean, user_mean, picked = spread(bits, rs, cs, item_shard, user_shard, queries, n_col)
+        item_mean, user_mean, picked = spread(mask_blk, item_shard, user_shard, queries, n_col)
         final_user, final_item, scores = score(user_mean, item_mean, picked)
         return final_user, final_item, scores
 

time: 207 us -> 201 us (0.971)
  Pallas kernels: 206 us -> 200 us
    pallas_call x1 -> x0, Pallas kernels: 43.3 us -> none  [pack(): pl.pallas_call(pack_kernel, in_specs=[anyspace], out_specs=[anyspace, vme...]
    pallas_call x1, Pallas kernels: 151 us -> 191 us  [spread(): pl.pallas_call(functools.partial(spread_kernel, n_col), in_specs=[anyspac...]
where the time goes in v4:
time: 201 us
  Pallas kernels  200 us (100%)
    pallas_call x1, Pallas kernels, spread(): pl.pallas_call(functools.partial(spread_kernel, n_col), in_specs=[anyspac...  191 us
    pallas_call x1, Pallas kernels, score(): pl.pallas_call(score_kernel, grid=(rows // tile,), in_specs=[whole, block...  9.57 us

profile of v4, /device:TPU:0, one launch (start us, length us, event | category | flops | bytes accessed | tf_op | source)
XLA Modules:
  0.0 200.9 jit_solution(12232780658595671230)
XLA Ops:
  0.6 190.7 %spread.1 = (bf16[8192,256]{1,0:T(8,128)(2,1)}, bf16[512,256]{1,0:T(8,128)(2,1)}, bf16[512,256]{1,0:T(8,128)(2,1)}) custom-call(s32[2048,16384]{1,0:T(8,128)} %mask.1, bf16[8192,256]{1,0:T(8,128)(2,1)} %item0.1, bf16[512,256]{1,0:T(8,128)(2,1)} %user0.1, s32[1,512]{1,0:T(1,128)} %bitcast.1), custom_call_target="tpu_custom_call" | custom-call | flops 103079215104 | bytes 134217728 | tf_op jit(solution)/shard_map/spread/pallas_call | solution.py:357
  191.4 9.6 %score.1 = (bf16[512,256]{1,0:T(8,128)(2,1)}, bf16[8192,256]{1,0:T(8,128)(2,1)}, f32[512,8192]{1,0:T(8,128)}) custom-call(bf16[512,256]{1,0:T(8,128)(2,1)} %get-tuple-element.6.user, bf16[8192,256]{1,0:T(8,128)(2,1)} %get-tuple-element.7.item, bf16[512,256]{1,0:T(8,128)(2,1)} %get-tuple-element.8.picked), custom_call_target="tpu_custom_call" | custom-call | tf_op jit(solution)/shard_map/score/pallas_call | solution.py:409
